TPU v7x, 32 devices: a whole 2x2x4 slice. The times are simulated.
32 devices in a mesh: groups: 2 (over y), blk: 4 (over z), sub: 4 (over x, core).
Axes of the slice: x: 2, y: 2, z: 4, core: 2. Of those that a mesh axis runs over, the one named last changes fastest.
Arguments:
- dense_coef: float32 [256, 128, 128], P(('groups', 'blk'), 'sub'), parts along dimension 0, may hold values from -6 to 6
- sparse_coef: float32 [8, 128, 128], P(('groups', 'blk'), 'sub'), parts along dimension 0, may hold values from -0.0234375 to 0.0234375
- pattern: int32 [8], P('groups'), parts along dimension 0, may hold values from 0 to 159, as said below
Outputs:
- product_coef: float32 [256, 128, 128], P(('groups', 'blk'), 'sub'), parts along dimension 0
There are 2 independent parts, one for each index of `groups`. A program takes and returns all parts, laid end to end along the dimension named above; each array names one. Nothing has to cross between parts.
Inputs may be any that keep to these rules, and one draw needn't show every extreme that they name: `pattern`: the 4 entries are distinct.
All inputs are finite; a program needn't handle non-finite values.
Results may differ from a plain program's by a relative error of at most 0.000076.
Values sent between devices are 32-bit elements; how exact they have to be, the bound alone decides.
No kernel may reach another device: no remote copies, remote signals or barrier semaphores. Data moves between devices by JAX's collectives and lax.ppermute only.
A program may use at most 128 MiB of HBM per device.

v0:
```python
import math

import jax
import jax.numpy as jnp
from jax import lax
from jax.sharding import PartitionSpec as P

STEPS = 5


exact_setting = lax.Precision.HIGHEST


def shifted(block, axis, distance):
    devices = range(lax.axis_size(axis))
    route = [((i - distance) % len(devices), i) for i in devices]
    return lax.ppermute(block, axis, route)


def angle_table(row_total, col_total, period, row_start, col_start):
    row_ids = jnp.arange(row_total, dtype=jnp.int32)[:, None] + row_start
    col_ids = jnp.arange(col_total, dtype=jnp.int32)[None, :] + col_start
    phases = jnp.mod(row_ids * col_ids, period).astype(jnp.float32) * (2.0 * math.pi / period)
    return (jnp.cos(phases), jnp.sin(phases))


def forward(series_coefficients):
    col_local = series_coefficients.shape[1]
    row_total = series_coefficients.shape[2]
    padded = 2 * row_total
    col_total = col_local * lax.axis_size("sub")
    period = padded * col_total
    cosine_lookup, sine_lookup = angle_table(row_total, padded, padded, 0, 0)
    initial_real = jnp.einsum(
        "ufz,ze->ufe", series_coefficients, cosine_lookup, precision=exact_setting
    )
    initial_imaginary = -jnp.einsum(
        "ufz,ze->ufe", series_coefficients, sine_lookup, precision=exact_setting
    )
    twist_cos, twist_sin = angle_table(
        col_local, padded, period, lax.axis_index("sub") * col_local, 0
    )
    turned_real = initial_real * twist_cos + initial_imaginary * twist_sin
    turned_imag = initial_imaginary * twist_cos - initial_real * twist_sin
    stacked = jnp.stack([turned_real, turned_imag], axis=0)
    outer_cosine, outer_sine = angle_table(col_total, col_total, col_total, 0, 0)
    halves = lax.all_to_all(stacked, "sub", split_axis=3, concat_axis=2, tiled=True)
    partial_real = halves[0]
    partial_imaginary = halves[1]
    output_real = jnp.einsum(
        "rxs,xl->rsl", partial_real, outer_cosine, precision=exact_setting
    ) + jnp.einsum("rxs,xl->rsl", partial_imaginary, outer_sine, precision=exact_setting)
    output_imaginary = jnp.einsum(
        "rxs,xl->rsl", partial_imaginary, outer_cosine, precision=exact_setting
    ) - jnp.einsum("rxs,xl->rsl", partial_real, outer_sine, precision=exact_setting)
    return jnp.stack([output_real, output_imaginary], axis=0)


def flatten(halves):
    return (halves[0].reshape(halves[0].shape[0], -1), halves[1].reshape(halves[1].shape[0], -1))


def accumulate(totals, source, sparse, pattern, start):
    source_len = source[0].shape[0]
    targets = jnp.arange(totals[0].shape[0], dtype=jnp.int32)

    def one_entry(entry, running):
        wanted = start + targets - pattern[entry]
        valid = jnp.logical_and(wanted >= 0, wanted < source_len)[:, None]
        safe = jnp.clip(wanted, 0, source_len - 1)
        src_real = jnp.where(valid, jnp.take(source[0], safe, axis=0), 0.0)
        src_imag = jnp.where(valid, jnp.take(source[1], safe, axis=0), 0.0)
        sp_real = sparse[0][entry][None, :]
        sp_imag = sparse[1][entry][None, :]
        return (
            running[0] + src_real * sp_real - src_imag * sp_imag,
            running[1] + src_real * sp_imag + src_imag * sp_real,
        )

    return lax.fori_loop(0, pattern.shape[0], one_entry, totals)


def inverse(totals, local_rows, col_total):
    block_count = totals[0].shape[0]
    spectrum_real = totals[0].reshape(block_count, local_rows, col_total)
    spectrum_imaginary = totals[1].reshape(block_count, local_rows, col_total)
    padded = local_rows * lax.axis_size("sub")
    period = padded * col_total
    outer_cosine, outer_sine = angle_table(col_total, col_total, col_total, 0, 0)
    combined_real = jnp.einsum(
        "ahz,zr->arh", spectrum_real, outer_cosine, precision=exact_setting
    ) - jnp.einsum("ahz,zr->arh", spectrum_imaginary, outer_sine, precision=exact_setting)
    combined_imaginary = jnp.einsum(
        "ahz,zr->arh", spectrum_real, outer_sine, precision=exact_setting
    ) + jnp.einsum("ahz,zr->arh", spectrum_imaginary, outer_cosine, precision=exact_setting)
    twist_cos, twist_sin = angle_table(
        col_total, local_rows, period, 0, lax.axis_index("sub") * local_rows
    )
    turned_real = combined_real * twist_cos - combined_imaginary * twist_sin
    turned_imag = combined_real * twist_sin + combined_imaginary * twist_cos
    inverse_step_real, inverse_step_imaginary = (
        lax.all_to_all(turned_real, "sub", split_axis=1, concat_axis=2, tiled=True),
        lax.all_to_all(turned_imag, "sub", split_axis=1, concat_axis=2, tiled=True),
    )
    closing_cosine, closing_sine = angle_table(padded, padded, padded, 0, 0)
    value_entries = jnp.einsum(
        "xmj,jo->xmo", inverse_step_real, closing_cosine, precision=exact_setting
    ) - jnp.einsum("xmj,jo->xmo", inverse_step_imaginary, closing_sine, precision=exact_setting)
    return value_entries / period


def local(dense_coef, sparse_coef, pattern):
    block_count = dense_coef.shape[0]
    row_total = dense_coef.shape[2]
    spectra = forward(dense_coef)
    spec_shape = spectra[0].shape
    sparse = flatten(lax.all_gather(forward(sparse_coef), "blk", axis=1, tiled=True))
    empty_sum = jnp.zeros((block_count, spec_shape[1] * spec_shape[2]), jnp.float32)
    totals = (empty_sum, empty_sum)
    current = spectra
    for turn_index in range(STEPS + 1):
        if turn_index > 0:
            current = shifted(current, "blk", 1)
        totals = accumulate(totals, flatten(current), sparse, pattern, turn_index * block_count)
    value_entries = inverse(totals, spec_shape[1], spec_shape[2])
    lower_half = value_entries[:, :, :row_total]
    upper_half = value_entries[:, :, row_total:]
    carried_in = shifted(upper_half[-1:], "blk", 1)
    return lower_half + jnp.concatenate([carried_in, upper_half[:-1]], axis=0)


def solution(mesh):
    return jax.shard_map(
        local,
        mesh=mesh,
        in_specs=(
            P(("groups", "blk"), "sub", None),
            P(("groups", "blk"), "sub", None),
            P("groups"),
        ),
        out_specs=P(("groups", "blk"), "sub", None),
        check_vma=False,
    )
```

profile of v0, /device:TPU:0, one launch (start us, length us, event | category | flops | bytes accessed | tf_op | source)
XLA Modules:
  0.0 462.3 jit_solution(10227931367806987062)
XLA Ops:
  6.1 4.2 all-to-all-start.1
  14.5 7.6 %copy.18 = f32[2,32,32,256]{2,1,0,3:T(8,128)} copy(f32[2,32,32,256]{3,2,1,0:T(8,128)S(1)} %pad_maximum_fusion) | data formatting | bytes 4194304 | tf_op jit(solution)/shard_map/stack | solution.py:45
  22.1 7.1 %reshape.364 = f32[4,1,131072]{2,1,0:T(1,128)} reshape(f32[256,2,32,32]{3,2,1,0:T(8,128)} %bitcast.225) | data formatting | bytes 4194304
  29.2 4.5 all-to-all-start
  36.8 15.2 %all_gather.3 = f32[2,4,64,128]{3,2,1,0:T(8,128)S(1)} all-gather(f32[2,1,64,128]{3,2,1,0:T(8,128)S(1)} %pad_maximum_fusion.3), channel_id=1, replica_groups=mesh['groups'=2,'blk'=4,'sub'=4] {'blk'}, dimensions={1}, use_global_device_ids=true | all-gather | bytes 327680 | tf_op jit(solution)/shard_map/all_gather | solution.py:117
  52.3 7.1 %all-to-all-done = f32[4,1,131072]{2,1,0:T(1,128)} async-done(((f32[4,1,131072]{2,1,0:T(1,128)}), f32[4,1,131072]{2,1,0:T(1,128)}, u32[]{:S(2)}, u32[]{:S(2)}) %all-to-all-start) | async-done | bytes 2097184 | tf_op jit(solution)/shard_map/all_to_all | solution.py:47
  59.4 7.7 %reduce = f32[4,131072]{1,0:T(4,128)S(1)} reduce(f32[4,1,131072]{2,1,0:T(1,128)} %all-to-all-done, f32[]{:T(128)} %broadcast.711), dimensions={1}, to_apply=%all_to_all.48.reduce_sub_computation | reduce | bytes 4194308 | tf_op jit(solution)/shard_map/all_to_all | solution.py:47
  67.1 6.2 %reshape.365 = f32[256,2,32,32]{3,2,1,0:T(8,128)} reshape(f32[4,131072]{1,0:T(4,128)S(1)} %reduce) | data formatting | bytes 4194304
  73.3 8.0 %copy.19 = f32[2,32,32,4,64]{4,2,3,1,0:T(8,128)} copy(f32[2,32,32,4,64]{2,1,0,4,3:T(8,128)} %bitcast.226) | data formatting | bytes 4194304 | tf_op jit(solution)/shard_map/all_to_all | solution.py:47
  103.1 36.4 %while.101 = (s32[]{:T(128)}, f32[32,8192]{1,0:T(8,128)S(1)}, f32[32,8192]{1,0:T(8,128)}, s32[4]{0:T(128)S(1)}, f32[32,8192]{1,0:T(8,128)S(1)}, /*index=5*/f32[4...) while((s32[]{:T(128)}, f32[32,8192]{1,0:T(8,128)S(1)}, ...), condition=%wide.region_1.3_spmd.clone, body=%wide.region_0.2_spmd.clone.sunk | while | flops 3671555 | bytes 10687239 | solution.py:80
  139.4 10.1 %collective-permute-done = f32[2,32,64,128]{3,2,1,0:T(8,128)} collective-permute-done((f32[2,32,64,128]{3,2,1,0:T(8,128)}, f32[2,32,64,128]{3,2,1,0:T(8,128)}, u32[]{:S(2)}, u32[]{:S(2)}) %collective-permute-start) | collective-permute-done | bytes 2097184 | tf_op jit(solution)/shard_map/ppermute | solution.py:17
  152.5 38.5 %while.96 = (s32[]{:T(128)}, f32[32,8192]{1,0:T(8,128)S(1)}, f32[32,8192]{1,0:T(8,128)}, s32[4]{0:T(128)S(1)}, f32[32,8192]{1,0:T(8,128)S(1)}, /*index=5*/f32[4,...) while((s32[]{:T(128)}, f32[32,8192]{1,0:T(8,128)S(1)}, ...), condition=%wide.region_3.5_spmd.clone, body=%wide.region_2.4_spmd.clone.sunk | while | flops 3147330 | bytes 10687221 | solution.py:80
  158.2 4.0 multiply_add_fusion.10
  167.8 4.0 multiply_add_fusion.10
  177.4 4.0 multiply_add_fusion.10
  187.1 4.0 multiply_add_fusion.10
  191.0 10.1 %collective-permute-done.1 = f32[2,32,64,128]{3,2,1,0:T(8,128)} collective-permute-done((f32[2,32,64,128]{3,2,1,0:T(8,128)}, f32[2,32,64,128]{3,2,1,0:T(8,128)}, u32[]{:S(2)}, u32[]{:S(2)}) %collective-permute-start.1) | collective-permute-done | bytes 2097184 | tf_op jit(solution)/shard_map/ppermute | solution.py:17
  204.1 38.9 %while.97 = (s32[]{:T(128)}, f32[32,8192]{1,0:T(8,128)S(1)}, f32[32,8192]{1,0:T(8,128)}, s32[4]{0:T(128)S(1)}, f32[32,8192]{1,0:T(8,128)S(1)}, /*index=5*/f32[4,...) while((s32[]{:T(128)}, f32[32,8192]{1,0:T(8,128)S(1)}, ...), condition=%wide.region_5.7_spmd.clone, body=%wide.region_4.6_spmd.clone.sunk | while | flops 3147330 | bytes 10687221 | solution.py:80
  210.1 4.0 multiply_add_fusion.11
  243.0 8.8 %collective-permute-done.2 = f32[2,32,64,128]{3,2,1,0:T(8,128)} collective-permute-done((f32[2,32,64,128]{3,2,1,0:T(8,128)}, f32[2,32,64,128]{3,2,1,0:T(8,128)}, u32[]{:S(2)}, u32[]{:S(2)}) %collective-permute-start.2) | collective-permute-done | bytes 2097184 | tf_op jit(solution)/shard_map/ppermute | solution.py:17
  254.7 38.5 %while.98 = (s32[]{:T(128)}, f32[32,8192]{1,0:T(8,128)S(1)}, f32[32,8192]{1,0:T(8,128)}, s32[4]{0:T(128)S(1)}, f32[32,8192]{1,0:T(8,128)S(1)}, /*index=5*/f32[4,...) while((s32[]{:T(128)}, f32[32,8192]{1,0:T(8,128)S(1)}, ...), condition=%wide.region_7.9_spmd.clone, body=%wide.region_6.8_spmd.clone.sunk | while | flops 3147330 | bytes 10687221 | solution.py:80
  293.3 8.4 %collective-permute-done.3 = f32[2,32,64,128]{3,2,1,0:T(8,128)} collective-permute-done((f32[2,32,64,128]{3,2,1,0:T(8,128)}, f32[2,32,64,128]{3,2,1,0:T(8,128)}, u32[]{:S(2)}, u32[]{:S(2)}) %collective-permute-start.3) | collective-permute-done | bytes 2097184 | tf_op jit(solution)/shard_map/ppermute | solution.py:17
  304.6 38.5 %while.99 = (s32[]{:T(128)}, f32[32,8192]{1,0:T(8,128)S(1)}, f32[32,8192]{1,0:T(8,128)}, s32[4]{0:T(128)S(1)}, f32[32,8192]{1,0:T(8,128)S(1)}, /*index=5*/f32[4,...) while((s32[]{:T(128)}, f32[32,8192]{1,0:T(8,128)S(1)}, ...), condition=%wide.region_9.11_spmd.clone, body=%wide.region_8.10_spmd.clone.sunk | while | flops 3147330 | bytes 10687221 | solution.py:80
  329.5 4.0 multiply_add_fusion.13
  339.1 4.0 multiply_add_fusion.13
  343.1 7.5 %collective-permute-done.4 = f32[2,32,64,128]{3,2,1,0:T(8,128)} collective-permute-done((f32[2,32,64,128]{3,2,1,0:T(8,128)}, f32[2,32,64,128]{3,2,1,0:T(8,128)}, u32[]{:S(2)}, u32[]{:S(2)}) %collective-permute-start.4) | collective-permute-done | bytes 2097184 | tf_op jit(solution)/shard_map/ppermute | solution.py:17
  353.5 38.7 %while.100 = (s32[]{:T(128)}, f32[32,8192]{1,0:T(8,128)S(1)}, f32[32,8192]{1,0:T(8,128)}, s32[4]{0:T(128)S(1)}, f32[32,8192]{1,0:T(8,128)S(1)}, /*index=5*/f32[4...) while((s32[]{:T(128)}, f32[32,8192]{1,0:T(8,128)S(1)}, ...), condition=%wide.region_11.13_spmd.clone, body=%wide.region_10.12_spmd.clone.sunk | while | flops 3147330 | bytes 10687221 | solution.py:80
  413.6 8.9 %all-to-all-done.2 = f32[4,1,65536]{2,1,0:T(1,128)S(1)} async-done(((f32[4,1,65536]{2,1,0:T(1,128)}), f32[4,1,65536]{2,1,0:T(1,128)S(1)}, u32[]{:S(2)}, u32[]{:S(2)}) %all-to-all-start.2) | async-done | bytes 1048608 | tf_op jit(solution)/shard_map/all_to_all | solution.py:102
  423.5 4.5 all-to-all-start.3
  428.0 4.6 %reduce.3 = f32[4,65536]{1,0:T(4,128)S(1)} reduce(f32[4,1,65536]{2,1,0:T(1,128)} %copy-done.4, f32[]{:T(128)} %broadcast.711), dimensions={1}, to_apply=%all_to_all.54.reduce_sub_computation | reduce | bytes 2097156 | tf_op jit(solution)/shard_map/all_to_all | solution.py:102
  442.5 4.6 %reduce.4 = f32[4,65536]{1,0:T(4,128)S(1)} reduce(f32[4,1,65536]{2,1,0:T(1,128)} %all-to-all-done.3, f32[]{:T(128)} %broadcast.711), dimensions={1}, to_apply=%all_to_all.58.reduce_sub_computation | reduce | bytes 2097156 | tf_op jit(solution)/shard_map/all_to_all | solution.py:103
  455.6 5.5 %collective-permute-done.5 = f32[1,32,128]{2,1,0:T(8,128)S(1)} collective-permute-done((f32[1,32,128]{2,1,0:T(8,128)S(1)}, f32[1,32,128]{2,1,0:T(8,128)S(1)}, u32[]{:S(2)}, u32[]{:S(2)}) %collective-permute-start.5) | collective-permute-done | bytes 16416 | tf_op jit(solution)/shard_map/ppermute | solution.py:17
  (274 shorter events, 291.7 us)
Async XLA Ops:
  0.0 10.4 %copy-start = (f32[32,32,128]{2,1,0:T(8,128)S(1)}, f32[32,32,128]{2,1,0:T(8,128)}, u32[]{:S(2)}) copy-start(f32[32,32,128]{2,1,0:T(8,128)} %param.17) | copy-start | bytes 1572868
  6.1 23.0 %all-to-all-start.1 = ((f32[4,1,4096]{2,1,0:T(1,128)}), f32[4,1,4096]{2,1,0:T(1,128)S(1)}, u32[]{:S(2)}, u32[]{:S(2)}) async-start(f32[4,1,4096]{2,1,0:T(1,128)} %reshape.366), calls=%async_computation.1 | async-start | bytes 131072 | tf_op jit(solution)/shard_map/all_to_all | solution.py:47
  29.2 30.2 %all-to-all-start = ((f32[4,1,131072]{2,1,0:T(1,128)}), f32[4,1,131072]{2,1,0:T(1,128)}, u32[]{:S(2)}, u32[]{:S(2)}) async-start(f32[4,1,131072]{2,1,0:T(1,128)} %reshape.364), calls=%async_computation | async-start | bytes 4194304 | tf_op jit(solution)/shard_map/all_to_all | solution.py:47
  99.8 49.8 %collective-permute-start = (f32[2,32,64,128]{3,2,1,0:T(8,128)}, f32[2,32,64,128]{3,2,1,0:T(8,128)}, u32[]{:S(2)}, u32[]{:S(2)}) collective-permute-start(f32[2,32,64,128]{3,2,1,0:T(8,128)} %pad_maximum_fusion.1), channel_id=1, source_target_pairs={{12,0},{0,4},{4,8},{8,12},{13,1},{1,5},{5,9},{9,13},{14,2},{2,6},{... | collective-permute-start | bytes 6291464 | tf_op jit(solution)/shard_map/ppermute | solution.py:17
  101.9 1.2 copy-start.7
  152.4 48.7 %collective-permute-start.1 = (f32[2,32,64,128]{3,2,1,0:T(8,128)}, f32[2,32,64,128]{3,2,1,0:T(8,128)}, u32[]{:S(2)}, u32[]{:S(2)}) collective-permute-start(f32[2,32,64,128]{3,2,1,0:T(8,128)} %collective-permute-done), channel_id=1, source_target_pairs={{12,0},{0,4},{4,8},{8,12},{13,1},{1,5},{5,9},{9,13},{14,2},{2,6},{... | collective-permute-start | bytes 6291464 | tf_op jit(solution)/shard_map/ppermute | solution.py:17
  204.0 47.8 %collective-permute-start.2 = (f32[2,32,64,128]{3,2,1,0:T(8,128)}, f32[2,32,64,128]{3,2,1,0:T(8,128)}, u32[]{:S(2)}, u32[]{:S(2)}) collective-permute-start(f32[2,32,64,128]{3,2,1,0:T(8,128)} %collective-permute-done.1), channel_id=1, source_target_pairs={{12,0},{0,4},{4,8},{8,12},{13,1},{1,5},{5,9},{9,13},{14,2},{2,6},{... | collective-permute-start | bytes 6291464 | tf_op jit(solution)/shard_map/ppermute | solution.py:17
  254.7 47.0 %collective-permute-start.3 = (f32[2,32,64,128]{3,2,1,0:T(8,128)}, f32[2,32,64,128]{3,2,1,0:T(8,128)}, u32[]{:S(2)}, u32[]{:S(2)}) collective-permute-start(f32[2,32,64,128]{3,2,1,0:T(8,128)} %collective-permute-done.2), channel_id=1, source_target_pairs={{12,0},{0,4},{4,8},{8,12},{13,1},{1,5},{5,9},{9,13},{14,2},{2,6},{... | collective-permute-start | bytes 6291464 | tf_op jit(solution)/shard_map/ppermute | solution.py:17
  304.5 46.1 %collective-permute-start.4 = (f32[2,32,64,128]{3,2,1,0:T(8,128)}, f32[2,32,64,128]{3,2,1,0:T(8,128)}, u32[]{:S(2)}, u32[]{:S(2)}) collective-permute-start(f32[2,32,64,128]{3,2,1,0:T(8,128)} %collective-permute-done.3), channel_id=1, source_target_pairs={{12,0},{0,4},{4,8},{8,12},{13,1},{1,5},{5,9},{9,13},{14,2},{2,6},{... | collective-permute-start | bytes 6291464 | tf_op jit(solution)/shard_map/ppermute | solution.py:17
  392.4 2.5 copy-start.2
  395.1 1.3 copy-start.5
  395.1 1.3 copy-start.6
  404.6 17.9 %all-to-all-start.2 = ((f32[4,1,65536]{2,1,0:T(1,128)}), f32[4,1,65536]{2,1,0:T(1,128)S(1)}, u32[]{:S(2)}, u32[]{:S(2)}) async-start(f32[4,1,65536]{2,1,0:T(1,128)} %reshape.368), calls=%async_computation.2 | async-start | bytes 2097152 | tf_op jit(solution)/shard_map/all_to_all | solution.py:102
  422.5 1.0 copy-start.4
  423.5 18.9 %all-to-all-start.3 = ((f32[4,1,65536]{2,1,0:T(1,128)}), f32[4,1,65536]{2,1,0:T(1,128)}, u32[]{:S(2)}, u32[]{:S(2)}) async-start(f32[4,1,65536]{2,1,0:T(1,128)} %reshape.370), calls=%async_computation.3 | async-start | bytes 2097152 | tf_op jit(solution)/shard_map/all_to_all | solution.py:103
  450.8 2.6 copy-start.3
  450.8 11.1 %copy-start.1 = (f32[32,32,128]{2,1,0:T(8,128)S(1)}, f32[32,32,128]{2,1,0:T(8,128)}, u32[]{:S(2)}) copy-start(f32[32,32,128]{2,1,0:T(8,128)} %param.17) | copy-start | bytes 1572868
  455.4 5.6 %collective-permute-start.5 = (f32[1,32,128]{2,1,0:T(8,128)S(1)}, f32[1,32,128]{2,1,0:T(8,128)S(1)}, u32[]{:S(2)}, u32[]{:S(2)}) collective-permute-start(f32[1,32,128]{2,1,0:T(8,128)S(1)} %slice.124), channel_id=1, source_target_pairs={{12,0},{0,4},{4,8},{8,12},{13,1},{1,5},{5,9},{9,13},{14,2},{2,6},{... | collective-permute-start | bytes 49160 | tf_op jit(solution)/shard_map/ppermute | solution.py:17
where the time goes:
time: 472 us; the launch traced here: 462 us
  local copies, waits for them, and re-layouts  179 us (38%)
  other arithmetic  147 us (31%)
  waiting for transfers between devices  66.8 us (14%)
  matrix products  33.3 us (7%)
  starting transfers between devices  19.1 us (4%)
  blocking collectives  15.2 us (3%)
    add x24, other arithmetic, one_entry(): running[1] + src_real * sp_imag + src_imag * sp_real  92.9 us
    ppermute x6, waiting for transfers between devices, shifted(): return lax.ppermute(block, axis, route)  50.3 us
    gather x24, local copies, waits for them, and re-layouts, one_entry(): src_real = jnp.where(valid, jnp.take(source[0], safe, axis=0), 0.0)  44.2 us
    gather x24, local copies, waits for them, and re-layouts, one_entry(): src_imag = jnp.where(valid, jnp.take(source[1], safe, axis=0), 0.0)  44 us
    unnamed x27, local copies, waits for them, and re-layouts  22.9 us
    and x24, other arithmetic, one_entry(): src_real = jnp.where(valid, jnp.take(source[0], safe, axis=0), 0.0)  15.8 us
    select_n x24, other arithmetic, one_entry(): src_real = jnp.where(valid, jnp.take(source[0], safe, axis=0), 0.0)  15.6 us
    all_gather x1, blocking collectives, local(): lax.all_gather(forward(sparse_coef), 'blk', axis=1, tiled=True)  15.2 us
  transfers between devices with their start and end apart: 10, of which 9 were waited for; matrix products, arithmetic and copies ran while one was open for 50% of the time, Pallas kernels for 0%

commit v1 on v0

v1 whole, which is shorter than its diff:
```python
import math

import jax
import jax.numpy as jnp
import numpy as np
from jax import lax
from jax.experimental import pallas as pl
from jax.experimental.pallas import tpu as pltpu
from jax.sharding import PartitionSpec as P

LANES = 128
AXES = ("blk", "sub")


def halves(table):
    high = jnp.asarray(table, jnp.float32).astype(jnp.bfloat16)
    low = (jnp.asarray(table, jnp.float32) - high.astype(jnp.float32)).astype(jnp.bfloat16)
    return high, low


def split(values):
    high = values.astype(jnp.bfloat16)
    return high, (values - high.astype(jnp.float32)).astype(jnp.bfloat16)


def product3(left, right, dims):
    dot = lambda a, b: lax.dot_general(a, b, (dims, ((), ())), preferred_element_type=jnp.float32)
    return dot(left[0], right[0]) + (dot(left[0], right[1]) + dot(left[1], right[0]))


def regroup(tiles, width):
    tiles = list(tiles)
    group = lax.broadcasted_iota(jnp.int32, tiles[0].shape, len(tiles[0].shape) - 1) // width
    axis = len(tiles[0].shape) - 1
    step = len(tiles) // 2
    while step:
        keep = (group & step) == 0
        for s in range(len(tiles)):
            if s & step:
                continue
            a, b = tiles[s], tiles[s | step]
            tiles[s] = jnp.where(keep, a, pltpu.roll(b, step * width, axis))
            tiles[s | step] = jnp.where(keep, pltpu.roll(a, LANES - step * width, axis), b)
        step //= 2
    return tiles


class Sizes:
    def __init__(self, dense, sparse, pattern, mesh_shape):
        self.z, self.subs = mesh_shape["blk"], mesh_shape["sub"]
        self.devices = self.z * self.subs
        self.blocks, self.q, self.rows = dense.shape
        self.entries = sparse.shape[0]
        self.all_entries = pattern.shape[0]
        self.nf = self.rows // self.devices
        self.tiles = self.blocks * self.q // LANES
        self.all_blocks = self.blocks * self.z


def tables(n):
    f = np.arange(n.rows) + 0.5
    r = np.arange(n.rows)
    q = np.arange(LANES)
    arm = 2 * math.pi * f[:, None] * r[None, :] / (2 * n.rows)
    order = lambda c, s: np.stack([c.reshape(n.devices, n.nf, -1), s.reshape(n.devices, n.nf, -1)], 1).reshape(2 * n.rows, -1)
    forward = order(np.cos(arm), -np.sin(arm))
    backward = order(np.cos(arm), -np.sin(arm)) / (n.rows * LANES)
    twist = 2 * math.pi * f[:, None] * q[None, :] / (2 * n.rows * LANES)
    twist = np.stack([np.cos(twist), -np.sin(twist)], 0).reshape(2, n.devices, n.nf, LANES)
    turn = 2 * math.pi * (q[:, None] * q[None, :] % LANES) / LANES
    c, s = np.cos(turn), np.sin(turn)
    dft = np.block([[c, -s], [s, c]])
    idft = np.block([[c, s], [-s, c]])
    return forward, backward, twist, dft, idft


def rows_to_slots(n, dense_ref, sparse_ref, high_ref, low_ref, out_ref):
    weights = (high_ref[...], low_ref[...])
    nf = n.nf
    contract = ((1,), (1,))
    group = LANES // n.q
    for t in range(n.tiles):
        part = dense_ref[t * group:(t + 1) * group].reshape(LANES, n.rows)
        slots = product3(weights, split(part), contract)
        for d in range(n.devices):
            for c in range(2):
                out_ref[d, c * n.tiles + t] = slots[(d * 2 + c) * nf:(d * 2 + c + 1) * nf]
    part = sparse_ref[...].reshape(n.entries * n.q, n.rows)
    slots = product3(weights, split(part), contract)
    width = n.entries * n.q
    for d in range(n.devices):
        pieces = [slots[(d * 2 + c) * nf:(d * 2 + c + 1) * nf] for c in range(2)]
        if 2 * width < LANES:
            pieces.append(jnp.zeros((nf, LANES - 2 * width), jnp.float32))
        out_ref[d, 2 * n.tiles] = jnp.concatenate(pieces, axis=1)


def middle(n, place_ref, pattern_ref, in_ref, twist_ref, dft_h, dft_l, idft_h, idft_l, out_ref, wave, spec):
    nf = n.nf
    me = place_ref[0]
    tc, ts = twist_ref[0, me], twist_ref[1, me]
    group = n.subs
    contract = ((1,), (0,))

    def store(index, re, im):
        wave[index, :, :LANES] = re * tc - im * ts
        wave[index, :, LANES:] = re * ts + im * tc

    for z in range(n.z):
        for t in range(n.tiles):
            re = regroup([in_ref[z * n.subs + s, t] for s in range(group)], n.q)
            im = regroup([in_ref[z * n.subs + s, n.tiles + t] for s in range(group)], n.q)
            for j in range(group):
                store(z * n.blocks + t * group + j, re[j], im[j])
        parts = [in_ref[z * n.subs + s, 2 * n.tiles] for s in range(group)]
        width = n.entries * n.q
        for e in range(n.entries):
            at = e * n.q
            re = jnp.concatenate([p[:, at:at + n.q] for p in parts], axis=1)
            im = jnp.concatenate([p[:, width + at:width + at + n.q] for p in parts], axis=1)
            store(n.all_blocks + z * n.entries + e, re, im)

    def transform(source, target, count, table):
        chunk = n.blocks
        starts = list(range(0, count, chunk))
        for at in starts:
            size = min(chunk, count - at)
            rows = source[at:at + size].reshape(size * nf, 2 * LANES)
            target[at:at + size] = product3(split(rows), table, contract).reshape(size, nf, 2 * LANES)

    transform(wave, spec, n.all_blocks + n.all_entries, (dft_h[...], dft_l[...]))

    shifts = [lax.rem(pattern_ref[e], n.all_blocks) for e in range(n.all_entries)]
    first = me * nf
    slot = lax.broadcasted_iota(jnp.int32, (nf, LANES), 0) + first
    sign = jnp.where(lax.rem(slot, 2) == 0, 1.0, -1.0).astype(jnp.float32)

    def convolved(k):
        re = jnp.zeros((nf, LANES), jnp.float32)
        im = jnp.zeros((nf, LANES), jnp.float32)
        for e in range(n.all_entries):
            j = k - shifts[e]
            j = jnp.where(j < 0, j + n.all_blocks, j)
            ar, ai = spec[j, :, :LANES], spec[j, :, LANES:]
            sr, si = spec[n.all_blocks + e, :, :LANES], spec[n.all_blocks + e, :, LANES:]
            re = re + ar * sr - ai * si
            im = im + ar * si + ai * sr
        return re, im

    def step(k, before):
        re, im = convolved(k)
        wave[k, :, :LANES] = re - sign * before[1]
        wave[k, :, LANES:] = im + sign * before[0]
        return re, im

    lax.fori_loop(0, n.all_blocks, step, convolved(n.all_blocks - 1), unroll=8)

    transform(wave, spec, n.all_blocks, (idft_h[...], idft_l[...]))

    for z in range(n.z):
        for t in range(n.tiles):
            re, im = [], []
            for j in range(group):
                index = z * n.blocks + t * group + j
                er, ei = spec[index, :, :LANES], spec[index, :, LANES:]
                re.append(er * tc + ei * ts)
                im.append(ei * tc - er * ts)
            for s, tile in enumerate(regroup(re, n.q)):
                out_ref[z * n.subs + s, t] = tile
            for s, tile in enumerate(regroup(im, n.q)):
                out_ref[z * n.subs + s, n.tiles + t] = tile


def slots_to_rows(n, in_ref, high_ref, low_ref, out_ref):
    weights = (high_ref[...], low_ref[...])
    group = LANES // n.q
    for t in range(n.tiles):
        pieces = [in_ref[d, c * n.tiles + t] for d in range(n.devices) for c in range(2)]
        slots = jnp.concatenate(pieces, axis=0)
        rows = product3(split(slots), weights, ((0,), (0,)))
        out_ref[t * group:(t + 1) * group] = rows.reshape(group, n.q, n.rows)


def solution(mesh):
    def local(dense, sparse, pattern):
        n = Sizes(dense, sparse, pattern, mesh.shape)
        forward, backward, twist, dft, idft = tables(n)
        place = (lax.axis_index("blk") * n.subs + lax.axis_index("sub")).reshape(1)
        scalar = pl.BlockSpec(memory_space=pltpu.SMEM)
        whole = pl.BlockSpec(memory_space=pltpu.VMEM)
        out = lambda *shape: jax.ShapeDtypeStruct(shape, jnp.float32)
        sent = pl.pallas_call(
            lambda *refs: rows_to_slots(n, *refs),
            out_shape=out(n.devices, 2 * n.tiles + 1, n.nf, LANES),
            in_specs=[whole] * 4, out_specs=whole, name="rows_to_slots",
        )(dense, sparse, *halves(forward))
        taken = lax.all_to_all(sent, AXES, 0, 0, tiled=True)
        mixed = pl.pallas_call(
            lambda *refs: middle(n, *refs),
            out_shape=out(n.devices, 2 * n.tiles, n.nf, LANES),
            in_specs=[scalar] * 2 + [whole] * 6, out_specs=whole, name="middle",
            scratch_shapes=[pltpu.VMEM((n.all_blocks + n.all_entries, n.nf, 2 * LANES), jnp.float32)] * 2,
        )(place, pattern, taken, jnp.asarray(twist, jnp.float32), *halves(dft), *halves(idft))
        back = lax.all_to_all(mixed, AXES, 0, 0, tiled=True)
        return pl.pallas_call(
            lambda *refs: slots_to_rows(n, *refs),
            out_shape=out(*dense.shape),
            in_specs=[whole] * 3, out_specs=whole, name="slots_to_rows",
        )(back, *halves(backward))

    return jax.shard_map(
        local,
        mesh=mesh,
        in_specs=(P(("groups", "blk"), "sub", None), P(("groups", "blk"), "sub", None), P("groups")),
        out_specs=P(("groups", "blk"), "sub", None),
        check_vma=False,
    )
```

time: 472 us -> 75.9 us (0.16); the launches traced: 462 us -> 75.1 us
  local copies, waits for them, and re-layouts: 179 us -> 0.99 us
  other arithmetic: 147 us -> 0 us
  waiting for transfers between devices: 66.8 us -> 23.9 us
  matrix products: 33.3 us -> 0 us
  blocking collectives: 15.2 us -> 31.9 us
  starting transfers between devices: 19.1 us -> 7.39 us
  Pallas kernels: 0 us -> 10.9 us
    add x27 -> x0, other arithmetic: 93.7 us -> none  [the longest x24 92.9 us: one_entry(): running[1] + src_real * sp_imag + src_imag * sp_real]
    gather x48 -> x0, local copies, waits for them, and re-layouts: 88.2 us -> none  [the longest x24 44.2 us: one_entry(): src_real = jnp.where(valid, jnp.take(source[0], safe, axis=0), 0.0)]
    ppermute x6 -> x0, waiting for transfers between devices: 50.3 us -> none  [shifted(): return lax.ppermute(block, axis, route)]
    dot_general x18 -> x0, matrix products: 33.3 us -> none  [the longest x2 4.15 us: forward(): jnp.einsum('rxs,xl->rsl', partial_real, outer_sine, precision=exact_setting)]
    all_to_all x0 -> x1, blocking collectives: none -> 31.9 us  [local(): back = lax.all_to_all(mixed, AXES, 0, 0, tiled=True)]
    unnamed x27 -> x2, local copies, waits for them, and re-layouts: 22.9 us -> 0.99 us
    all_to_all x7 -> x0, local copies, waits for them, and re-layouts: 19.5 us -> none  [the longest x3 8.75 us: forward(): lax.all_to_all(stacked, 'sub', split_axis=3, concat_axis=2, tiled=True)]
    all_to_all x4 -> x0, other arithmetic: 17.9 us -> none  [the longest x2 8.59 us: forward(): lax.all_to_all(stacked, 'sub', split_axis=3, concat_axis=2, tiled=True)]
  transfers between devices with their start and end apart: 10 -> 1, of which waited for: 9 -> 1; matrix products, arithmetic and copies ran while one was open for 50% -> 0% of each run, Pallas kernels for 0% -> 0%
where the time goes in v1:
time: 75.9 us; the launch traced here: 75.1 us
  blocking collectives  31.9 us (42%)
  waiting for transfers between devices  23.9 us (31%)
  Pallas kernels  10.9 us (14%)
  starting transfers between devices  7.39 us (10%)
  local copies, waits for them, and re-layouts  0.99 us (1%)
    all_to_all x1, blocking collectives, local(): back = lax.all_to_all(mixed, AXES, 0, 0, tiled=True)  31.9 us
    all_to_all x1, waiting for transfers between devices, local(): taken = lax.all_to_all(sent, AXES, 0, 0, tiled=True)  23.9 us
    all_to_all x1, starting transfers between devices, local(): taken = lax.all_to_all(sent, AXES, 0, 0, tiled=True)  7.39 us
    pallas_call x1, Pallas kernels, local(): pl.pallas_call(lambda *refs: middle(n, *refs), out_shape=out(n.devices, 2...  5.43 us
    pallas_call x1, Pallas kernels, local(): pl.pallas_call(lambda *refs: rows_to_slots(n, *refs), out_shape=out(n.dev...  2.75 us
    pallas_call x1, Pallas kernels, local(): pl.pallas_call(lambda *refs: slots_to_rows(n, *refs), out_shape=out(*dens...  2.69 us
  transfers between devices with their start and end apart: 1, of which 1 were waited for; matrix products, arithmetic and copies ran while one was open for 0% of the time, Pallas kernels for 0%

profile of v1, /device:TPU:0, one launch (start us, length us, event | category | flops | bytes accessed | tf_op | source)
XLA Modules:
  0.0 75.1 jit_solution(74844495353459190)
XLA Ops:
  0.0 2.8 %rows_to_slots.1 = f32[16,17,8,128]{3,2,1,0:T(8,128)} custom-call(f32[32,32,128]{2,1,0:T(8,128)} %refs_0_.1, f32[1,32,128]{2,1,0:T(8,128)} %refs_1_.2, bf16[256,128]{1,0:T(8,128)(2,1)} %constant.25.refs_2_, bf16[256,128]{1,0:T(8,128)(2,1)} %constant.28.refs_3_), custom_call_target="tpu_custom_call" | custom-call | tf_op jit(solution)/shard_map/rows_to_slots/pallas_call | solution.py:192
  2.8 7.4 %all-to-all-start = ((f32[16,17,8,128]{3,2,1,0:T(8,128)}), f32[16,17,8,128]{3,2,1,0:T(8,128)S(1)}, u32[]{:S(2)}, u32[]{:S(2)}) async-start(f32[16,17,8,128]{3,2,1,0:T(8,128)} %rows_to_slots.1), calls=%async_computation | async-start | bytes 2228224 | tf_op jit(solution)/shard_map/all_to_all | solution.py:197
  10.2 23.9 %all-to-all-done.refs_2_ = f32[16,17,8,128]{3,2,1,0:T(8,128)S(1)} async-done(((f32[16,17,8,128]{3,2,1,0:T(8,128)}), f32[16,17,8,128]{3,2,1,0:T(8,128)S(1)}, u32[]{:S(2)}, u32[]{:S(2)}) %all-to-all-start) | async-done | bytes 1114144 | tf_op jit(solution)/shard_map/all_to_all | solution.py:197
  34.1 0.0 copy-start
  34.1 1.0 %copy-done = f32[16,17,8,128]{3,2,1,0:T(8,128)} copy-done((f32[16,17,8,128]{3,2,1,0:T(8,128)}, f32[16,17,8,128]{3,2,1,0:T(8,128)S(1)}, u32[]{:S(2)}) %copy-start) | copy-done | bytes 1114136
  35.1 5.4 %middle.1 = f32[16,16,8,128]{3,2,1,0:T(8,128)} custom-call(s32[1]{0:T(128)} %bitcast.refs_0_, s32[4]{0:T(128)} %refs_1_.3, f32[16,17,8,128]{3,2,1,0:T(8,128)} %copy-done, f32[2,16,8,128]{3,2,1,0:T(8,128)} %constant.20.clone.refs_3_, bf16[256,256]{1,0:T(8,128)(2,1)} %constant.29.refs_4_, bf16[256,256]{1,0:T(8,128)(2,1)} %constant.32.refs_5_, ...), custom_call_target="tpu_custom_call" | custom-call | tf_op jit(solution)/shard_map/middle/pallas_call | solution.py:198
  40.5 31.9 %all_to_all.10.refs_0_ = f32[16,16,8,128]{3,2,1,0:T(8,128)} all-to-all(f32[16,16,8,128]{3,2,1,0:T(8,128)} %middle.1), channel_id=1, replica_groups=mesh['groups'=2,'blk'=4,'sub'=4] {'blk','sub'}, dimensions={0} | all-to-all | bytes 2097152 | tf_op jit(solution)/shard_map/all_to_all | solution.py:204
  72.4 2.7 %slots_to_rows.1 = f32[32,32,128]{2,1,0:T(8,128)} custom-call(f32[16,16,8,128]{3,2,1,0:T(8,128)} %all_to_all.10.refs_0_, bf16[256,128]{1,0:T(8,128)(2,1)} %constant.37.refs_1_, bf16[256,128]{1,0:T(8,128)(2,1)} %constant.40.refs_2_), custom_call_target="tpu_custom_call" | custom-call | tf_op jit(solution)/shard_map/slots_to_rows/pallas_call | solution.py:205
Async XLA Ops:
  2.8 31.3 %all-to-all-start = ((f32[16,17,8,128]{3,2,1,0:T(8,128)}), f32[16,17,8,128]{3,2,1,0:T(8,128)S(1)}, u32[]{:S(2)}, u32[]{:S(2)}) async-start(f32[16,17,8,128]{3,2,1,0:T(8,128)} %rows_to_slots.1), calls=%async_computation | async-start | bytes 2228224 | tf_op jit(solution)/shard_map/all_to_all | solution.py:197
  34.1 1.0 %copy-start = (f32[16,17,8,128]{3,2,1,0:T(8,128)}, f32[16,17,8,128]{3,2,1,0:T(8,128)S(1)}, u32[]{:S(2)}) copy-start(f32[16,17,8,128]{3,2,1,0:T(8,128)S(1)} %all-to-all-done.refs_2_) | copy-start | bytes 3342340

commit v2 on v1

--- a/solution.py
+++ b/solution.py
@@ -9,12 +9,14 @@
 from jax.sharding import PartitionSpec as P
 
 LANES = 128
+GRANT = pltpu.CompilerParams(vmem_limit_bytes=16 * 2**20)
 AXES = ("blk", "sub")
 
 
 def halves(table):
-    high = jnp.asarray(table, jnp.float32).astype(jnp.bfloat16)
-    low = (jnp.asarray(table, jnp.float32) - high.astype(jnp.float32)).astype(jnp.bfloat16)
+    table = np.asarray(table, np.float32)
+    high = table.astype(jnp.bfloat16)
+    low = (table - high.astype(np.float32)).astype(jnp.bfloat16)
     return high, low
 
 
@@ -74,20 +76,32 @@
     return forward, backward, twist, dft, idft
 
 
-def rows_to_slots(n, dense_ref, sparse_ref, high_ref, low_ref, out_ref):
-    weights = (high_ref[...], low_ref[...])
+def rows_to_slots(n, dense_hbm, sparse_hbm, weights_hbm, out_ref, dense, sparse, weights, sems):
     nf = n.nf
     contract = ((1,), (1,))
     group = LANES // n.q
-    for t in range(n.tiles):
-        part = dense_ref[t * group:(t + 1) * group].reshape(LANES, n.rows)
-        slots = product3(weights, split(part), contract)
-        for d in range(n.devices):
-            for c in range(2):
-                out_ref[d, c * n.tiles + t] = slots[(d * 2 + c) * nf:(d * 2 + c + 1) * nf]
-    part = sparse_ref[...].reshape(n.entries * n.q, n.rows)
-    slots = product3(weights, split(part), contract)
     width = n.entries * n.q
+    steps = min(4, n.tiles)
+    per = n.tiles // steps
+    loads = [pltpu.make_async_copy(weights_hbm, weights, sems.at[0])]
+    for s in range(steps):
+        part = pl.ds(s * per * group, per * group)
+        loads.append(pltpu.make_async_copy(dense_hbm.at[part], dense.at[part], sems.at[1 + s]))
+    loads.append(pltpu.make_async_copy(sparse_hbm, sparse, sems.at[1 + steps]))
+    for load in loads:
+        load.start()
+    loads[0].wait()
+    table = (weights[0], weights[1])
+    for s in range(steps):
+        loads[1 + s].wait()
+        for t in range(s * per, (s + 1) * per):
+            part = dense[t * group:(t + 1) * group].reshape(LANES, n.rows)
+            slots = product3(table, split(part), contract)
+            for d in range(n.devices):
+                for c in range(2):
+                    out_ref[d, c * n.tiles + t] = slots[(d * 2 + c) * nf:(d * 2 + c + 1) * nf]
+    loads[-1].wait()
+    slots = product3(table, split(sparse[...].reshape(width, n.rows)), contract)
     for d in range(n.devices):
         pieces = [slots[(d * 2 + c) * nf:(d * 2 + c + 1) * nf] for c in range(2)]
         if 2 * width < LANES:
@@ -95,9 +109,9 @@
         out_ref[d, 2 * n.tiles] = jnp.concatenate(pieces, axis=1)
 
 
-def middle(n, place_ref, pattern_ref, in_ref, twist_ref, dft_h, dft_l, idft_h, idft_l, out_ref, wave, spec):
+def middle(n, pattern_ref, in_ref, twist_ref, dft_h, dft_l, idft_h, idft_l, out_ref, wave, spec):
     nf = n.nf
-    me = place_ref[0]
+    me = lax.axis_index("blk") * n.subs + lax.axis_index("sub")
     tc, ts = twist_ref[0, me], twist_ref[1, me]
     group = n.subs
     contract = ((1,), (0,))
@@ -140,7 +154,10 @@
         im = jnp.zeros((nf, LANES), jnp.float32)
         for e in range(n.all_entries):
             j = k - shifts[e]
-            j = jnp.where(j < 0, j + n.all_blocks, j)
+            if n.all_blocks & (n.all_blocks - 1) == 0:
+                j = j & (n.all_blocks - 1)
+            else:
+                j = jnp.where(j < 0, j + n.all_blocks, j)
             ar, ai = spec[j, :, :LANES], spec[j, :, LANES:]
             sr, si = spec[n.all_blocks + e, :, :LANES], spec[n.all_blocks + e, :, LANES:]
             re = re + ar * sr - ai * si
@@ -171,42 +188,57 @@
                 out_ref[z * n.subs + s, n.tiles + t] = tile
 
 
-def slots_to_rows(n, in_ref, high_ref, low_ref, out_ref):
-    weights = (high_ref[...], low_ref[...])
+def slots_to_rows(n, in_ref, weights_ref, out_hbm, rows_ref, sems):
+    weights = (weights_ref[0], weights_ref[1])
     group = LANES // n.q
-    for t in range(n.tiles):
-        pieces = [in_ref[d, c * n.tiles + t] for d in range(n.devices) for c in range(2)]
-        slots = jnp.concatenate(pieces, axis=0)
-        rows = product3(split(slots), weights, ((0,), (0,)))
-        out_ref[t * group:(t + 1) * group] = rows.reshape(group, n.q, n.rows)
+    steps = min(4, n.tiles)
+    per = n.tiles // steps
+    stores = []
+    for s in range(steps):
+        for t in range(s * per, (s + 1) * per):
+            pieces = [in_ref[d, c * n.tiles + t] for d in range(n.devices) for c in range(2)]
+            slots = jnp.concatenate(pieces, axis=0)
+            rows = product3(split(slots), weights, ((0,), (0,)))
+            rows_ref[t * group:(t + 1) * group] = rows.reshape(group, n.q, n.rows)
+        part = pl.ds(s * per * group, per * group)
+        stores.append(pltpu.make_async_copy(rows_ref.at[part], out_hbm.at[part], sems.at[s]))
+        stores[-1].start()
+    for store in stores:
+        store.wait()
 
 
 def solution(mesh):
     def local(dense, sparse, pattern):
         n = Sizes(dense, sparse, pattern, mesh.shape)
         forward, backward, twist, dft, idft = tables(n)
-        place = (lax.axis_index("blk") * n.subs + lax.axis_index("sub")).reshape(1)
         scalar = pl.BlockSpec(memory_space=pltpu.SMEM)
         whole = pl.BlockSpec(memory_space=pltpu.VMEM)
         out = lambda *shape: jax.ShapeDtypeStruct(shape, jnp.float32)
+        hbm = pl.BlockSpec(memory_space=pltpu.HBM)
+        steps = min(4, n.tiles)
         sent = pl.pallas_call(
             lambda *refs: rows_to_slots(n, *refs),
-            out_shape=out(n.devices, 2 * n.tiles + 1, n.nf, LANES),
-            in_specs=[whole] * 4, out_specs=whole, name="rows_to_slots",
-        )(dense, sparse, *halves(forward))
+            out_shape=pltpu.VMEM((n.devices, 2 * n.tiles + 1, n.nf, LANES), jnp.float32),
+            in_specs=[hbm] * 3, out_specs=whole, name="rows_to_slots", compiler_params=GRANT,
+            scratch_shapes=[
+                pltpu.VMEM(dense.shape, jnp.float32), pltpu.VMEM(sparse.shape, jnp.float32),
+                pltpu.VMEM((2, *forward.shape), jnp.bfloat16), pltpu.SemaphoreType.DMA((steps + 2,)),
+            ],
+        )(*(pltpu.with_memory_space_constraint(v, pltpu.HBM) for v in (dense, sparse, jnp.stack([jnp.asarray(h) for h in halves(forward)]))))
         taken = lax.all_to_all(sent, AXES, 0, 0, tiled=True)
         mixed = pl.pallas_call(
             lambda *refs: middle(n, *refs),
             out_shape=out(n.devices, 2 * n.tiles, n.nf, LANES),
-            in_specs=[scalar] * 2 + [whole] * 6, out_specs=whole, name="middle",
+            in_specs=[scalar] + [whole] * 6, out_specs=whole, name="middle", compiler_params=GRANT,
             scratch_shapes=[pltpu.VMEM((n.all_blocks + n.all_entries, n.nf, 2 * LANES), jnp.float32)] * 2,
-        )(place, pattern, taken, jnp.asarray(twist, jnp.float32), *halves(dft), *halves(idft))
+        )(pattern, taken, jnp.asarray(twist, jnp.float32), *halves(dft), *halves(idft))
         back = lax.all_to_all(mixed, AXES, 0, 0, tiled=True)
         return pl.pallas_call(
             lambda *refs: slots_to_rows(n, *refs),
             out_shape=out(*dense.shape),
-            in_specs=[whole] * 3, out_specs=whole, name="slots_to_rows",
-        )(back, *halves(backward))
+            in_specs=[whole] * 2, out_specs=hbm, name="slots_to_rows", compiler_params=GRANT,
+            scratch_shapes=[pltpu.VMEM(dense.shape, jnp.float32), pltpu.SemaphoreType.DMA((steps,))],
+        )(back, np.stack(halves(backward)))
 
     return jax.shard_map(
         local,

time: 75.9 us -> 71.3 us (0.939)
  blocking collectives: 31.9 us -> 63.5 us
  waiting for transfers between devices: 23.9 us -> 0 us
  starting transfers between devices: 7.39 us -> 0 us
  Pallas kernels: 10.9 us -> 6.97 us
  local copies, waits for them, and re-layouts: 0.99 us -> 0.05 us
    all_to_all x0 -> x1, blocking collectives: none -> 35.8 us  [local(): taken = lax.all_to_all(sent, AXES, 0, 0, tiled=True)]
    all_to_all x1 -> x0, waiting for transfers between devices: 23.9 us -> none  [local(): taken = lax.all_to_all(sent, AXES, 0, 0, tiled=True)]
    all_to_all x1 -> x0, starting transfers between devices: 7.39 us -> none  [local(): taken = lax.all_to_all(sent, AXES, 0, 0, tiled=True)]
    all_to_all x1, blocking collectives: 31.9 us -> 27.7 us  [local(): back = lax.all_to_all(mixed, AXES, 0, 0, tiled=True)]
    pallas_call x1, Pallas kernels: 5.43 us -> 3.25 us  [local(): pl.pallas_call(lambda *refs: middle(n, *refs), out_shape=out(n.devices, 2...]
    pallas_call x1, Pallas kernels: 2.69 us -> 1.32 us  [local(): pl.pallas_call(lambda *refs: slots_to_rows(n, *refs), out_shape=out(*dens...]
    unnamed x2 -> x14, local copies, waits for them, and re-layouts: 0.99 us -> 0.05 us
  transfers between devices with their start and end apart: 1 -> 0, of which waited for: 1 -> 0; matrix products, arithmetic and copies ran while one was open for 0% -> 0% of each run, Pallas kernels for 0% -> 0%
where the time goes in v2:
time: 71.3 us; the launch traced here: 70.6 us
  blocking collectives  63.5 us (89%)
  Pallas kernels  6.97 us (10%)
    all_to_all x1, blocking collectives, local(): taken = lax.all_to_all(sent, AXES, 0, 0, tiled=True)  35.8 us
    all_to_all x1, blocking collectives, local(): back = lax.all_to_all(mixed, AXES, 0, 0, tiled=True)  27.7 us
    pallas_call x1, Pallas kernels, local(): pl.pallas_call(lambda *refs: middle(n, *refs), out_shape=out(n.devices, 2...  3.25 us
    pallas_call x1, Pallas kernels, local(): pl.pallas_call(lambda *refs: rows_to_slots(n, *refs), out_shape=pltpu.VME...  2.4 us

profile of v2, /device:TPU:0, one launch (start us, length us, event | category | flops | bytes accessed | tf_op | source)
XLA Modules:
  0.0 70.6 jit_solution(16782473384955630287)
XLA Ops:
  0.0 2.4 %rows_to_slots.1 = f32[16,17,8,128]{3,2,1,0:T(8,128)S(1)} custom-call(f32[32,32,128]{2,1,0:T(8,128)} %refs_0_.2, f32[1,32,128]{2,1,0:T(8,128)} %refs_1_.2, bf16[2,256,128]{2,1,0:T(8,128)(2,1)} %constant.27.refs_2_), custom_call_target="tpu_custom_call" | custom-call | tf_op jit(solution)/shard_map/rows_to_slots/pallas_call | solution.py:219
  2.4 0.0 copy-start
  2.4 0.0 copy-start.1
  2.4 0.0 copy-start.2
  2.4 0.0 copy-start.3
  2.5 0.0 copy-start.4
  2.5 0.0 copy-start.6
  2.5 35.8 %all_to_all.10.refs_1_ = f32[16,17,8,128]{3,2,1,0:T(8,128)S(1)} all-to-all(f32[16,17,8,128]{3,2,1,0:T(8,128)S(1)} %rows_to_slots.1), channel_id=1, replica_groups=mesh['groups'=2,'blk'=4,'sub'=4] {'blk','sub'}, dimensions={0} | all-to-all | bytes 2228224 | tf_op jit(solution)/shard_map/all_to_all | solution.py:228
  38.3 0.0 copy-done
  38.3 0.0 copy-done.1
  38.3 0.0 copy-done.2
  38.3 0.0 copy-done.3
  38.3 0.0 copy-done.4
  38.3 0.0 copy-done.6
  38.3 3.2 %middle.1 = f32[16,16,8,128]{3,2,1,0:T(8,128)S(1)} custom-call(s32[4]{0:T(128)S(1)} %copy-done.6, f32[16,17,8,128]{3,2,1,0:T(8,128)S(1)} %all_to_all.10.refs_1_, f32[2,16,8,128]{3,2,1,0:T(8,128)S(1)} %copy-done.4, bf16[256,256]{1,0:T(8,128)(2,1)S(1)} %copy-done.3, bf16[256,256]{1,0:T(8,128)(2,1)S(1)} %copy-done.2, bf16[256,256]{1,0:T(8,128)(2,1)S(1)} %copy-done.1, ...), custom_call_target="tpu_custom_call" | custom-call | tf_op jit(solution)/shard_map/middle/pallas_call | solution.py:229
  41.6 0.0 copy-start.5
  41.6 27.7 %all_to_all.11.refs_0_ = f32[16,16,8,128]{3,2,1,0:T(8,128)S(1)} all-to-all(f32[16,16,8,128]{3,2,1,0:T(8,128)S(1)} %middle.1), channel_id=1, replica_groups=mesh['groups'=2,'blk'=4,'sub'=4] {'blk','sub'}, dimensions={0} | all-to-all | bytes 2097152 | tf_op jit(solution)/shard_map/all_to_all | solution.py:235
  69.2 0.0 copy-done.5
  69.3 1.3 %slots_to_rows.1 = f32[32,32,128]{2,1,0:T(8,128)} custom-call(f32[16,16,8,128]{3,2,1,0:T(8,128)S(1)} %all_to_all.11.refs_0_, bf16[2,256,128]{2,1,0:T(8,128)(2,1)S(1)} %copy-done.5), custom_call_target="tpu_custom_call" | custom-call | tf_op jit(solution)/shard_map/slots_to_rows/pallas_call | solution.py:236
Async XLA Ops:
  2.4 35.9 %copy-start = (bf16[256,256]{1,0:T(8,128)(2,1)S(1)}, bf16[256,256]{1,0:T(8,128)(2,1)}, u32[]{:S(2)}) copy-start(bf16[256,256]{1,0:T(8,128)(2,1)} %constant.22.clone.refs_6_) | copy-start | bytes 393220
  2.4 35.9 %copy-start.1 = (bf16[256,256]{1,0:T(8,128)(2,1)S(1)}, bf16[256,256]{1,0:T(8,128)(2,1)}, u32[]{:S(2)}) copy-start(bf16[256,256]{1,0:T(8,128)(2,1)} %constant.21.clone.refs_5_) | copy-start | bytes 393220
  2.4 35.8 %copy-start.2 = (bf16[256,256]{1,0:T(8,128)(2,1)S(1)}, bf16[256,256]{1,0:T(8,128)(2,1)}, u32[]{:S(2)}) copy-start(bf16[256,256]{1,0:T(8,128)(2,1)} %constant.20.clone.refs_4_) | copy-start | bytes 393220
  2.4 35.8 %copy-start.3 = (bf16[256,256]{1,0:T(8,128)(2,1)S(1)}, bf16[256,256]{1,0:T(8,128)(2,1)}, u32[]{:S(2)}) copy-start(bf16[256,256]{1,0:T(8,128)(2,1)} %constant.19.clone.refs_3_) | copy-start | bytes 393220
  2.5 35.8 %copy-start.4 = (f32[2,16,8,128]{3,2,1,0:T(8,128)S(1)}, f32[2,16,8,128]{3,2,1,0:T(8,128)}, u32[]{:S(2)}) copy-start(f32[2,16,8,128]{3,2,1,0:T(8,128)} %constant.18.clone.refs_2_) | copy-start | bytes 393220
  2.5 35.8 %copy-start.6 = (s32[4]{0:T(128)S(1)}, s32[4]{0:T(128)}, u32[]{:S(2)}) copy-start(s32[4]{0:T(128)} %refs_0_.3) | copy-start | bytes 52
  41.6 27.7 %copy-start.5 = (bf16[2,256,128]{2,1,0:T(8,128)(2,1)S(1)}, bf16[2,256,128]{2,1,0:T(8,128)(2,1)}, u32[]{:S(2)}) copy-start(bf16[2,256,128]{2,1,0:T(8,128)(2,1)} %constant.23.clone.refs_1_) | copy-start | bytes 393220

commit v3 on v2

--- a/solution.py
+++ b/solution.py
@@ -91,22 +91,33 @@
     for load in loads:
         load.start()
     loads[0].wait()
-    table = (weights[0], weights[1])
+    table = weights[...]
+
+    def slots_of(rows):
+        high, low = split(rows)
+        both = jnp.concatenate([high, low], axis=1)
+        dot = lambda x, y: lax.dot_general(x, y, (contract, ((), ())), preferred_element_type=jnp.float32)
+        return dot(table[:, :2 * n.rows], both) + dot(table[:, 2 * n.rows:], high)
+
     for s in range(steps):
         loads[1 + s].wait()
-        for t in range(s * per, (s + 1) * per):
-            part = dense[t * group:(t + 1) * group].reshape(LANES, n.rows)
-            slots = product3(table, split(part), contract)
+        slots = slots_of(dense[s * per * group:(s + 1) * per * group].reshape(per * LANES, n.rows))
+        for i in range(per):
+            t = s * per + i
             for d in range(n.devices):
                 for c in range(2):
-                    out_ref[d, c * n.tiles + t] = slots[(d * 2 + c) * nf:(d * 2 + c + 1) * nf]
+                    rows = slice((d * 2 + c) * nf, (d * 2 + c + 1) * nf)
+                    out_ref[d, c * n.tiles + t] = slots[rows, i * LANES:(i + 1) * LANES]
     loads[-1].wait()
-    slots = product3(table, split(sparse[...].reshape(width, n.rows)), contract)
+    slots = slots_of(sparse[...].reshape(width, n.rows))
     for d in range(n.devices):
         pieces = [slots[(d * 2 + c) * nf:(d * 2 + c + 1) * nf] for c in range(2)]
         if 2 * width < LANES:
             pieces.append(jnp.zeros((nf, LANES - 2 * width), jnp.float32))
         out_ref[d, 2 * n.tiles] = jnp.concatenate(pieces, axis=1)
+
+
+RUN = 8
 
 
 def middle(n, pattern_ref, in_ref, twist_ref, dft_h, dft_l, idft_h, idft_l, out_ref, wave, spec):
@@ -115,71 +126,101 @@
     tc, ts = twist_ref[0, me], twist_ref[1, me]
     group = n.subs
     contract = ((1,), (0,))
+    base = n.all_entries
+    width = n.entries * n.q
 
     def store(index, re, im):
         wave[index, :, :LANES] = re * tc - im * ts
         wave[index, :, LANES:] = re * ts + im * tc
 
-    for z in range(n.z):
+    def transform(at, count, table):
+        rows = wave[at:at + count].reshape(count * nf, 2 * LANES)
+        return product3(split(rows), table, contract).reshape(count, nf, 2 * LANES)
+
+    def gather(z):
+        if z == 0:
+            for y in range(n.z):
+                parts = [in_ref[y * n.subs + s, 2 * n.tiles] for s in range(group)]
+                for e in range(n.entries):
+                    at = e * n.q
+                    re = jnp.concatenate([p[:, at:at + n.q] for p in parts], axis=1)
+                    im = jnp.concatenate([p[:, width + at:width + at + n.q] for p in parts], axis=1)
+                    store(y * n.entries + e, re, im)
         for t in range(n.tiles):
             re = regroup([in_ref[z * n.subs + s, t] for s in range(group)], n.q)
             im = regroup([in_ref[z * n.subs + s, n.tiles + t] for s in range(group)], n.q)
             for j in range(group):
-                store(z * n.blocks + t * group + j, re[j], im[j])
-        parts = [in_ref[z * n.subs + s, 2 * n.tiles] for s in range(group)]
-        width = n.entries * n.q
-        for e in range(n.entries):
-            at = e * n.q
-            re = jnp.concatenate([p[:, at:at + n.q] for p in parts], axis=1)
-            im = jnp.concatenate([p[:, width + at:width + at + n.q] for p in parts], axis=1)
-            store(n.all_blocks + z * n.entries + e, re, im)
-
-    def transform(source, target, count, table):
-        chunk = n.blocks
-        starts = list(range(0, count, chunk))
-        for at in starts:
-            size = min(chunk, count - at)
-            rows = source[at:at + size].reshape(size * nf, 2 * LANES)
-            target[at:at + size] = product3(split(rows), table, contract).reshape(size, nf, 2 * LANES)
-
-    transform(wave, spec, n.all_blocks + n.all_entries, (dft_h[...], dft_l[...]))
+                store(base + z * n.blocks + t * group + j, re[j], im[j])
+
+    def forward(z):
+        at = base + z * n.blocks if z else 0
+        count = n.blocks if z else base + n.blocks
+        result = transform(at, count, (dft_h[...], dft_l[...]))
+        re, im = result[:, :, :LANES], result[:, :, LANES:]
+        spec[at:at + count, :, :LANES] = re
+        spec[at:at + count, :, LANES:2 * LANES] = im
+        spec[at:at + count, :, 2 * LANES:] = re + im
+
+    gather(0)
+    for z in range(1, n.z):
+        gather(z)
+        forward(z - 1)
+    forward(n.z - 1)
+    spec[base + n.all_blocks:base + n.all_blocks + RUN] = spec[base:base + RUN]
 
     shifts = [lax.rem(pattern_ref[e], n.all_blocks) for e in range(n.all_entries)]
-    first = me * nf
-    slot = lax.broadcasted_iota(jnp.int32, (nf, LANES), 0) + first
+    slot = lax.broadcasted_iota(jnp.int32, (nf, LANES), 0) + me * nf
     sign = jnp.where(lax.rem(slot, 2) == 0, 1.0, -1.0).astype(jnp.float32)
 
-    def convolved(k):
-        re = jnp.zeros((nf, LANES), jnp.float32)
-        im = jnp.zeros((nf, LANES), jnp.float32)
+    def factors():
+        out = []
         for e in range(n.all_entries):
-            j = k - shifts[e]
-            if n.all_blocks & (n.all_blocks - 1) == 0:
-                j = j & (n.all_blocks - 1)
-            else:
-                j = jnp.where(j < 0, j + n.all_blocks, j)
-            ar, ai = spec[j, :, :LANES], spec[j, :, LANES:]
-            sr, si = spec[n.all_blocks + e, :, :LANES], spec[n.all_blocks + e, :, LANES:]
-            re = re + ar * sr - ai * si
-            im = im + ar * si + ai * sr
-        return re, im
-
-    def step(k, before):
-        re, im = convolved(k)
-        wave[k, :, :LANES] = re - sign * before[1]
-        wave[k, :, LANES:] = im + sign * before[0]
-        return re, im
-
-    lax.fori_loop(0, n.all_blocks, step, convolved(n.all_blocks - 1), unroll=8)
-
-    transform(wave, spec, n.all_blocks, (idft_h[...], idft_l[...]))
-
-    for z in range(n.z):
+            sr, si = spec[e, :, :LANES], spec[e, :, LANES:2 * LANES]
+            out.append((sr, si + sr, si - sr))
+        return out
+
+    def starts(k):
+        out = []
+        for shift in shifts:
+            j = k - shift
+            out.append(base + jnp.where(j < 0, j + n.all_blocks, j))
+        return out
+
+    def convolved(rows, i, table):
+        t = u = v = None
+        for e, (sr, ssum, sdiff) in enumerate(table):
+            at = rows[e] + i
+            a = spec[at, :, 2 * LANES:] * sr
+            b = spec[at, :, LANES:2 * LANES] * ssum
+            c = spec[at, :, :LANES] * sdiff
+            t, u, v = (a, b, c) if t is None else (t + a, u + b, v + c)
+        return t - u, t + v
+
+    def run_of(k, before, table):
+        rows = starts(k)
+        for i in range(RUN):
+            re, im = convolved(rows, i, table)
+            wave[k + i, :, :LANES] = re - sign * before[1]
+            wave[k + i, :, LANES:] = im + sign * before[0]
+            before = (re, im)
+        return before
+
+    def convolve(z, before):
+        if n.all_blocks * n.all_entries <= 1024:
+            table = factors()
+            for k in range(z * n.blocks, (z + 1) * n.blocks, RUN):
+                before = run_of(k, before, table)
+            return before
+        return lax.fori_loop(
+            0, n.blocks // RUN,
+            lambda i, carry: run_of(z * n.blocks + i * RUN, carry, factors()), before)
+
+    def scatter(z):
+        result = transform(z * n.blocks, n.blocks, (idft_h[...], idft_l[...]))
         for t in range(n.tiles):
             re, im = [], []
             for j in range(group):
-                index = z * n.blocks + t * group + j
-                er, ei = spec[index, :, :LANES], spec[index, :, LANES:]
+                er, ei = result[t * group + j, :, :LANES], result[t * group + j, :, LANES:]
                 re.append(er * tc + ei * ts)
                 im.append(ei * tc - er * ts)
             for s, tile in enumerate(regroup(re, n.q)):
@@ -187,18 +228,28 @@
             for s, tile in enumerate(regroup(im, n.q)):
                 out_ref[z * n.subs + s, n.tiles + t] = tile
 
+    before = convolved(starts(n.all_blocks - 1), 0, factors())
+    before = convolve(0, before)
+    for z in range(1, n.z):
+        before = convolve(z, before)
+        scatter(z - 1)
+    scatter(n.z - 1)
+
 
 def slots_to_rows(n, in_ref, weights_ref, out_hbm, rows_ref, sems):
-    weights = (weights_ref[0], weights_ref[1])
+    both = weights_ref[...]
+    first = both[:, :n.rows]
     group = LANES // n.q
-    steps = min(4, n.tiles)
+    steps = min(8, n.tiles)
     per = n.tiles // steps
+    dot = lambda a, b: lax.dot_general(a, b, (((0,), (0,)), ((), ())), preferred_element_type=jnp.float32)
     stores = []
     for s in range(steps):
         for t in range(s * per, (s + 1) * per):
             pieces = [in_ref[d, c * n.tiles + t] for d in range(n.devices) for c in range(2)]
-            slots = jnp.concatenate(pieces, axis=0)
-            rows = product3(split(slots), weights, ((0,), (0,)))
+            high, low = split(jnp.concatenate(pieces, axis=0))
+            wide = dot(high, both)
+            rows = wide[:, :n.rows] + (wide[:, n.rows:] + dot(low, first))
             rows_ref[t * group:(t + 1) * group] = rows.reshape(group, n.q, n.rows)
         part = pl.ds(s * per * group, per * group)
         stores.append(pltpu.make_async_copy(rows_ref.at[part], out_hbm.at[part], sems.at[s]))
@@ -216,29 +267,34 @@
         out = lambda *shape: jax.ShapeDtypeStruct(shape, jnp.float32)
         hbm = pl.BlockSpec(memory_space=pltpu.HBM)
         steps = min(4, n.tiles)
+        high, low = halves(forward)
+        table = np.concatenate([high, high, low], axis=1)
         sent = pl.pallas_call(
             lambda *refs: rows_to_slots(n, *refs),
             out_shape=pltpu.VMEM((n.devices, 2 * n.tiles + 1, n.nf, LANES), jnp.float32),
             in_specs=[hbm] * 3, out_specs=whole, name="rows_to_slots", compiler_params=GRANT,
             scratch_shapes=[
                 pltpu.VMEM(dense.shape, jnp.float32), pltpu.VMEM(sparse.shape, jnp.float32),
-                pltpu.VMEM((2, *forward.shape), jnp.bfloat16), pltpu.SemaphoreType.DMA((steps + 2,)),
+                pltpu.VMEM((2 * n.rows, 3 * n.rows), jnp.bfloat16), pltpu.SemaphoreType.DMA((steps + 2,)),
             ],
-        )(*(pltpu.with_memory_space_constraint(v, pltpu.HBM) for v in (dense, sparse, jnp.stack([jnp.asarray(h) for h in halves(forward)]))))
+        )(*(pltpu.with_memory_space_constraint(v, pltpu.HBM) for v in (dense, sparse, jnp.asarray(table))))
         taken = lax.all_to_all(sent, AXES, 0, 0, tiled=True)
         mixed = pl.pallas_call(
             lambda *refs: middle(n, *refs),
             out_shape=out(n.devices, 2 * n.tiles, n.nf, LANES),
             in_specs=[scalar] + [whole] * 6, out_specs=whole, name="middle", compiler_params=GRANT,
-            scratch_shapes=[pltpu.VMEM((n.all_blocks + n.all_entries, n.nf, 2 * LANES), jnp.float32)] * 2,
+            scratch_shapes=[
+                pltpu.VMEM((n.all_entries + n.all_blocks, n.nf, 2 * LANES), jnp.float32),
+                pltpu.VMEM((n.all_entries + n.all_blocks + RUN, n.nf, 3 * LANES), jnp.float32),
+            ],
         )(pattern, taken, jnp.asarray(twist, jnp.float32), *halves(dft), *halves(idft))
         back = lax.all_to_all(mixed, AXES, 0, 0, tiled=True)
         return pl.pallas_call(
             lambda *refs: slots_to_rows(n, *refs),
             out_shape=out(*dense.shape),
             in_specs=[whole] * 2, out_specs=hbm, name="slots_to_rows", compiler_params=GRANT,
-            scratch_shapes=[pltpu.VMEM(dense.shape, jnp.float32), pltpu.SemaphoreType.DMA((steps,))],
-        )(back, np.stack(halves(backward)))
+            scratch_shapes=[pltpu.VMEM(dense.shape, jnp.float32), pltpu.SemaphoreType.DMA((min(8, n.tiles),))],
+        )(back, np.concatenate(halves(backward), axis=1))
 
     return jax.shard_map(
         local,

time: 71.3 us -> 70.8 us (level)
  no operation moved by 1% of the time
where the time goes in v3:
time: 70.8 us; the launch traced here: 70.1 us
  blocking collectives  63.4 us (90%)
  Pallas kernels  6.52 us (9%)
    all_to_all x1, blocking collectives, local(): taken = lax.all_to_all(sent, AXES, 0, 0, tiled=True)  35.8 us
    all_to_all x1, blocking collectives, local(): back = lax.all_to_all(mixed, AXES, 0, 0, tiled=True)  27.7 us
    pallas_call x1, Pallas kernels, local(): pl.pallas_call(lambda *refs: middle(n, *refs), out_shape=out(n.devices, 2...  2.89 us
    pallas_call x1, Pallas kernels, local(): pl.pallas_call(lambda *refs: rows_to_slots(n, *refs), out_shape=pltpu.VME...  2.45 us

profile of v3, /device:TPU:0, one launch (start us, length us, event | category | flops | bytes accessed | tf_op | source)
XLA Modules:
  0.0 70.1 jit_solution(16214761950187417162)
XLA Ops:
  0.0 2.5 %rows_to_slots.1 = f32[16,17,8,128]{3,2,1,0:T(8,128)S(1)} custom-call(f32[32,32,128]{2,1,0:T(8,128)} %refs_0_.2, f32[1,32,128]{2,1,0:T(8,128)} %refs_1_.2, bf16[256,384]{1,0:T(8,128)(2,1)} %constant.14.clone.refs_2_), custom_call_target="tpu_custom_call" | custom-call | tf_op jit(solution)/shard_map/rows_to_slots/pallas_call | solution.py:272
  2.5 0.0 copy-start
  2.5 0.0 copy-start.1
  2.5 0.0 copy-start.2
  2.5 0.0 copy-start.3
  2.5 0.0 copy-start.4
  2.5 0.0 copy-start.6
  2.5 35.8 %all_to_all.10.refs_1_ = f32[16,17,8,128]{3,2,1,0:T(8,128)S(1)} all-to-all(f32[16,17,8,128]{3,2,1,0:T(8,128)S(1)} %rows_to_slots.1), channel_id=1, replica_groups=mesh['groups'=2,'blk'=4,'sub'=4] {'blk','sub'}, dimensions={0} | all-to-all | bytes 2228224 | tf_op jit(solution)/shard_map/all_to_all | solution.py:281
  38.3 0.0 copy-done
  38.3 0.0 copy-done.1
  38.3 0.0 copy-done.2
  38.3 0.0 copy-done.3
  38.3 0.0 copy-done.4
  38.3 0.0 copy-done.6
  38.4 2.9 %middle.1 = f32[16,16,8,128]{3,2,1,0:T(8,128)S(1)} custom-call(s32[4]{0:T(128)S(1)} %copy-done.6, f32[16,17,8,128]{3,2,1,0:T(8,128)S(1)} %all_to_all.10.refs_1_, f32[2,16,8,128]{3,2,1,0:T(8,128)S(1)} %copy-done.4, bf16[256,256]{1,0:T(8,128)(2,1)S(1)} %copy-done.3, bf16[256,256]{1,0:T(8,128)(2,1)S(1)} %copy-done.2, bf16[256,256]{1,0:T(8,128)(2,1)S(1)} %copy-done.1, ...), custom_call_target="tpu_custom_call" | custom-call | tf_op jit(solution)/shard_map/middle/pallas_call | solution.py:282
  41.3 0.0 copy-start.5
  41.3 27.7 %all_to_all.11.refs_0_ = f32[16,16,8,128]{3,2,1,0:T(8,128)S(1)} all-to-all(f32[16,16,8,128]{3,2,1,0:T(8,128)S(1)} %middle.1), channel_id=1, replica_groups=mesh['groups'=2,'blk'=4,'sub'=4] {'blk','sub'}, dimensions={0} | all-to-all | bytes 2097152 | tf_op jit(solution)/shard_map/all_to_all | solution.py:291
  68.9 0.0 copy-done.5
  68.9 1.2 %slots_to_rows.1 = f32[32,32,128]{2,1,0:T(8,128)} custom-call(f32[16,16,8,128]{3,2,1,0:T(8,128)S(1)} %all_to_all.11.refs_0_, bf16[256,256]{1,0:T(8,128)(2,1)S(1)} %copy-done.5), custom_call_target="tpu_custom_call" | custom-call | tf_op jit(solution)/shard_map/slots_to_rows/pallas_call | solution.py:292
Async XLA Ops:
  2.5 35.9 %copy-start = (bf16[256,256]{1,0:T(8,128)(2,1)S(1)}, bf16[256,256]{1,0:T(8,128)(2,1)}, u32[]{:S(2)}) copy-start(bf16[256,256]{1,0:T(8,128)(2,1)} %constant.19.clone.refs_6_) | copy-start | bytes 393220
  2.5 35.8 %copy-start.1 = (bf16[256,256]{1,0:T(8,128)(2,1)S(1)}, bf16[256,256]{1,0:T(8,128)(2,1)}, u32[]{:S(2)}) copy-start(bf16[256,256]{1,0:T(8,128)(2,1)} %constant.18.clone.refs_5_) | copy-start | bytes 393220
  2.5 35.8 %copy-start.2 = (bf16[256,256]{1,0:T(8,128)(2,1)S(1)}, bf16[256,256]{1,0:T(8,128)(2,1)}, u32[]{:S(2)}) copy-start(bf16[256,256]{1,0:T(8,128)(2,1)} %constant.17.clone.refs_4_) | copy-start | bytes 393220
  2.5 35.8 %copy-start.3 = (bf16[256,256]{1,0:T(8,128)(2,1)S(1)}, bf16[256,256]{1,0:T(8,128)(2,1)}, u32[]{:S(2)}) copy-start(bf16[256,256]{1,0:T(8,128)(2,1)} %constant.16.clone.refs_3_) | copy-start | bytes 393220
  2.5 35.8 %copy-start.4 = (f32[2,16,8,128]{3,2,1,0:T(8,128)S(1)}, f32[2,16,8,128]{3,2,1,0:T(8,128)}, u32[]{:S(2)}) copy-start(f32[2,16,8,128]{3,2,1,0:T(8,128)} %constant.15.clone.refs_2_) | copy-start | bytes 393220
  2.5 35.8 %copy-start.6 = (s32[4]{0:T(128)S(1)}, s32[4]{0:T(128)}, u32[]{:S(2)}) copy-start(s32[4]{0:T(128)} %refs_0_.3) | copy-start | bytes 52
  41.3 27.7 %copy-start.5 = (bf16[256,256]{1,0:T(8,128)(2,1)S(1)}, bf16[256,256]{1,0:T(8,128)(2,1)}, u32[]{:S(2)}) copy-start(bf16[256,256]{1,0:T(8,128)(2,1)} %constant.20.clone.refs_1_) | copy-start | bytes 393220

commit v4 on v3

--- a/solution.py
+++ b/solution.py
@@ -31,20 +31,15 @@
 
 
 def regroup(tiles, width):
+    count = len(tiles)
+    group = lax.broadcasted_iota(jnp.int32, tiles[0].shape, len(tiles[0].shape) - 1) // width
     tiles = list(tiles)
-    group = lax.broadcasted_iota(jnp.int32, tiles[0].shape, len(tiles[0].shape) - 1) // width
-    axis = len(tiles[0].shape) - 1
-    step = len(tiles) // 2
-    while step:
+    step = 1
+    while step < count:
         keep = (group & step) == 0
-        for s in range(len(tiles)):
-            if s & step:
-                continue
-            a, b = tiles[s], tiles[s | step]
-            tiles[s] = jnp.where(keep, a, pltpu.roll(b, step * width, axis))
-            tiles[s | step] = jnp.where(keep, pltpu.roll(a, LANES - step * width, axis), b)
-        step //= 2
-    return tiles
+        tiles = [jnp.where(keep, tiles[m], tiles[(m + step) % count]) for m in range(count)]
+        step *= 2
+    return [tiles[-j % count] for j in range(count)]
 
 
 class Sizes:
@@ -73,7 +68,9 @@
     c, s = np.cos(turn), np.sin(turn)
     dft = np.block([[c, -s], [s, c]])
     idft = np.block([[c, s], [-s, c]])
-    return forward, backward, twist, dft, idft
+    phase = 2 * math.pi * (np.arange(n.subs)[:, None] * q[None, :] % n.subs) / n.subs
+    phase = np.stack([np.cos(phase), -np.sin(phase)], 0).reshape(2, n.subs, 1, LANES)
+    return forward, backward, phase, twist, dft, idft
 
 
 def rows_to_slots(n, dense_hbm, sparse_hbm, weights_hbm, out_ref, dense, sparse, weights, sems):
@@ -92,6 +89,7 @@
         load.start()
     loads[0].wait()
     table = weights[...]
+    me = lax.axis_index("sub")
 
     def slots_of(rows):
         high, low = split(rows)
@@ -101,7 +99,11 @@
 
     for s in range(steps):
         loads[1 + s].wait()
-        slots = slots_of(dense[s * per * group:(s + 1) * per * group].reshape(per * LANES, n.rows))
+        rows = [
+            dense[t * group + lax.rem(g - me + group, group)]
+            for t in range(s * per, (s + 1) * per) for g in range(group)
+        ]
+        slots = slots_of(jnp.concatenate(rows, axis=0))
         for i in range(per):
             t = s * per + i
             for d in range(n.devices):
@@ -120,16 +122,17 @@
 RUN = 8
 
 
-def middle(n, pattern_ref, in_ref, twist_ref, dft_h, dft_l, idft_h, idft_l, out_ref, wave, spec):
+def middle(n, pattern_ref, in_ref, phase_ref, twist_ref, dft_h, dft_l, idft_h, idft_l, out_ref, wave, spec):
     nf = n.nf
     me = lax.axis_index("blk") * n.subs + lax.axis_index("sub")
-    tc, ts = twist_ref[0, me], twist_ref[1, me]
     group = n.subs
+    turned = [[twist_ref[c, me] if j == 0 else pltpu.roll(twist_ref[c, me], j * n.q, 1) for c in range(2)] for j in range(group)]
     contract = ((1,), (0,))
     base = n.all_entries
     width = n.entries * n.q
 
-    def store(index, re, im):
+    def store(index, re, im, j=0):
+        tc, ts = turned[j]
         wave[index, :, :LANES] = re * tc - im * ts
         wave[index, :, LANES:] = re * ts + im * tc
 
@@ -150,7 +153,7 @@
             re = regroup([in_ref[z * n.subs + s, t] for s in range(group)], n.q)
             im = regroup([in_ref[z * n.subs + s, n.tiles + t] for s in range(group)], n.q)
             for j in range(group):
-                store(base + z * n.blocks + t * group + j, re[j], im[j])
+                store(base + z * n.blocks + t * group + j, re[j], im[j], j)
 
     def forward(z):
         at = base + z * n.blocks if z else 0
@@ -171,11 +174,15 @@
     shifts = [lax.rem(pattern_ref[e], n.all_blocks) for e in range(n.all_entries)]
     slot = lax.broadcasted_iota(jnp.int32, (nf, LANES), 0) + me * nf
     sign = jnp.where(lax.rem(slot, 2) == 0, 1.0, -1.0).astype(jnp.float32)
+    over_re, over_im = -sign * phase_ref[1, 1], sign * phase_ref[0, 1]
 
     def factors():
         out = []
         for e in range(n.all_entries):
-            sr, si = spec[e, :, :LANES], spec[e, :, LANES:2 * LANES]
+            xr, xi = spec[e, :, :LANES], spec[e, :, LANES:2 * LANES]
+            power = lax.rem(shifts[e], group)
+            pr, pi = phase_ref[0, power], phase_ref[1, power]
+            sr, si = xr * pr - xi * pi, xr * pi + xi * pr
             out.append((sr, si + sr, si - sr))
         return out
 
@@ -200,8 +207,8 @@
         rows = starts(k)
         for i in range(RUN):
             re, im = convolved(rows, i, table)
-            wave[k + i, :, :LANES] = re - sign * before[1]
-            wave[k + i, :, LANES:] = im + sign * before[0]
+            wave[k + i, :, :LANES] = re + (over_re * before[0] - over_im * before[1])
+            wave[k + i, :, LANES:] = im + (over_re * before[1] + over_im * before[0])
             before = (re, im)
         return before
 
@@ -220,6 +227,7 @@
         for t in range(n.tiles):
             re, im = [], []
             for j in range(group):
+                tc, ts = turned[j]
                 er, ei = result[t * group + j, :, :LANES], result[t * group + j, :, LANES:]
                 re.append(er * tc + ei * ts)
                 im.append(ei * tc - er * ts)
@@ -240,6 +248,7 @@
     both = weights_ref[...]
     first = both[:, :n.rows]
     group = LANES // n.q
+    me = lax.axis_index("sub")
     steps = min(8, n.tiles)
     per = n.tiles // steps
     dot = lambda a, b: lax.dot_general(a, b, (((0,), (0,)), ((), ())), preferred_element_type=jnp.float32)
@@ -250,7 +259,8 @@
             high, low = split(jnp.concatenate(pieces, axis=0))
             wide = dot(high, both)
             rows = wide[:, :n.rows] + (wide[:, n.rows:] + dot(low, first))
-            rows_ref[t * group:(t + 1) * group] = rows.reshape(group, n.q, n.rows)
+            for g in range(group):
+                rows_ref[t * group + lax.rem(g - me + group, group)] = rows[g * n.q:(g + 1) * n.q]
         part = pl.ds(s * per * group, per * group)
         stores.append(pltpu.make_async_copy(rows_ref.at[part], out_hbm.at[part], sems.at[s]))
         stores[-1].start()
@@ -261,7 +271,7 @@
 def solution(mesh):
     def local(dense, sparse, pattern):
         n = Sizes(dense, sparse, pattern, mesh.shape)
-        forward, backward, twist, dft, idft = tables(n)
+        forward, backward, phase, twist, dft, idft = tables(n)
         scalar = pl.BlockSpec(memory_space=pltpu.SMEM)
         whole = pl.BlockSpec(memory_space=pltpu.VMEM)
         out = lambda *shape: jax.ShapeDtypeStruct(shape, jnp.float32)
@@ -282,12 +292,12 @@
         mixed = pl.pallas_call(
             lambda *refs: middle(n, *refs),
             out_shape=out(n.devices, 2 * n.tiles, n.nf, LANES),
-            in_specs=[scalar] + [whole] * 6, out_specs=whole, name="middle", compiler_params=GRANT,
+            in_specs=[scalar] + [whole] * 7, out_specs=whole, name="middle", compiler_params=GRANT,
             scratch_shapes=[
                 pltpu.VMEM((n.all_entries + n.all_blocks, n.nf, 2 * LANES), jnp.float32),
                 pltpu.VMEM((n.all_entries + n.all_blocks + RUN, n.nf, 3 * LANES), jnp.float32),
             ],
-        )(pattern, taken, jnp.asarray(twist, jnp.float32), *halves(dft), *halves(idft))
+        )(pattern, taken, jnp.asarray(phase, jnp.float32), jnp.asarray(twist, jnp.float32), *halves(dft), *halves(idft))
         back = lax.all_to_all(mixed, AXES, 0, 0, tiled=True)
         return pl.pallas_call(
             lambda *refs: slots_to_rows(n, *refs),

time: 70.8 us -> 70.3 us (level)
  no operation moved by 1% of the time
where the time goes in v4:
time: 70.3 us; the launch traced here: 69.6 us
  blocking collectives  63.4 us (90%)
  Pallas kernels  5.94 us (8%)
    all_to_all x1, blocking collectives, local(): taken = lax.all_to_all(sent, AXES, 0, 0, tiled=True)  35.8 us
    all_to_all x1, blocking collectives, local(): back = lax.all_to_all(mixed, AXES, 0, 0, tiled=True)  27.7 us
    pallas_call x1, Pallas kernels, local(): pl.pallas_call(lambda *refs: rows_to_slots(n, *refs), out_shape=pltpu.VME...  2.45 us
    pallas_call x1, Pallas kernels, local(): pl.pallas_call(lambda *refs: middle(n, *refs), out_shape=out(n.devices, 2...  2.31 us

profile of v4, /device:TPU:0, one launch (start us, length us, event | category | flops | bytes accessed | tf_op | source)
XLA Modules:
  0.0 69.6 jit_solution(2241797541567373417)
XLA Ops:
  0.0 2.5 %rows_to_slots.1 = f32[16,17,8,128]{3,2,1,0:T(8,128)S(1)} custom-call(f32[32,32,128]{2,1,0:T(8,128)} %refs_0_.2, f32[1,32,128]{2,1,0:T(8,128)} %refs_1_.2, bf16[256,384]{1,0:T(8,128)(2,1)} %constant.16.clone.refs_2_), custom_call_target="tpu_custom_call" | custom-call | tf_op jit(solution)/shard_map/rows_to_slots/pallas_call | solution.py:282
  2.5 0.0 copy-start
  2.5 0.0 copy-start.1
  2.5 0.0 copy-start.2
  2.5 0.0 copy-start.3
  2.5 0.0 copy-start.4
  2.5 0.0 copy-start.6
  2.5 0.0 copy-start.7
  2.5 35.8 %all_to_all.10.refs_1_ = f32[16,17,8,128]{3,2,1,0:T(8,128)S(1)} all-to-all(f32[16,17,8,128]{3,2,1,0:T(8,128)S(1)} %rows_to_slots.1), channel_id=1, replica_groups=mesh['groups'=2,'blk'=4,'sub'=4] {'blk','sub'}, dimensions={0} | all-to-all | bytes 2228224 | tf_op jit(solution)/shard_map/all_to_all | solution.py:291
  38.3 0.0 copy-done
  38.3 0.0 copy-done.1
  38.3 0.0 copy-done.2
  38.3 0.0 copy-done.3
  38.4 0.0 copy-done.4
  38.4 0.0 copy-done.6
  38.4 0.0 copy-done.7
  38.4 2.3 %middle.1 = f32[16,16,8,128]{3,2,1,0:T(8,128)S(1)} custom-call(s32[4]{0:T(128)S(1)} %copy-done.7, f32[16,17,8,128]{3,2,1,0:T(8,128)S(1)} %all_to_all.10.refs_1_, f32[2,4,1,128]{3,2,1,0:T(1,128)S(1)} %copy-done.6, f32[2,16,8,128]{3,2,1,0:T(8,128)S(1)} %copy-done.4, bf16[256,256]{1,0:T(8,128)(2,1)S(1)} %copy-done.3, bf16[256,256]{1,0:T(8,128)(2,1)S(1)} %copy-done.2, ...), custom_call_target="tpu_custom_call" | custom-call | tf_op jit(solution)/shard_map/middle/pallas_call | solution.py:292
  40.7 0.0 copy-start.5
  40.7 27.7 %all_to_all.11.refs_0_ = f32[16,16,8,128]{3,2,1,0:T(8,128)S(1)} all-to-all(f32[16,16,8,128]{3,2,1,0:T(8,128)S(1)} %middle.1), channel_id=1, replica_groups=mesh['groups'=2,'blk'=4,'sub'=4] {'blk','sub'}, dimensions={0} | all-to-all | bytes 2097152 | tf_op jit(solution)/shard_map/all_to_all | solution.py:301
  68.4 0.0 copy-done.5
  68.4 1.2 %slots_to_rows.1 = f32[32,32,128]{2,1,0:T(8,128)} custom-call(f32[16,16,8,128]{3,2,1,0:T(8,128)S(1)} %all_to_all.11.refs_0_, bf16[256,256]{1,0:T(8,128)(2,1)S(1)} %copy-done.5), custom_call_target="tpu_custom_call" | custom-call | tf_op jit(solution)/shard_map/slots_to_rows/pallas_call | solution.py:302
Async XLA Ops:
  2.5 35.9 %copy-start = (bf16[256,256]{1,0:T(8,128)(2,1)S(1)}, bf16[256,256]{1,0:T(8,128)(2,1)}, u32[]{:S(2)}) copy-start(bf16[256,256]{1,0:T(8,128)(2,1)} %constant.22.clone.refs_7_) | copy-start | bytes 393220
  2.5 35.9 %copy-start.1 = (bf16[256,256]{1,0:T(8,128)(2,1)S(1)}, bf16[256,256]{1,0:T(8,128)(2,1)}, u32[]{:S(2)}) copy-start(bf16[256,256]{1,0:T(8,128)(2,1)} %constant.21.clone.refs_6_) | copy-start | bytes 393220
  2.5 35.9 %copy-start.2 = (bf16[256,256]{1,0:T(8,128)(2,1)S(1)}, bf16[256,256]{1,0:T(8,128)(2,1)}, u32[]{:S(2)}) copy-start(bf16[256,256]{1,0:T(8,128)(2,1)} %constant.20.clone.refs_5_) | copy-start | bytes 393220
  2.5 35.8 %copy-start.3 = (bf16[256,256]{1,0:T(8,128)(2,1)S(1)}, bf16[256,256]{1,0:T(8,128)(2,1)}, u32[]{:S(2)}) copy-start(bf16[256,256]{1,0:T(8,128)(2,1)} %constant.19.clone.refs_4_) | copy-start | bytes 393220
  2.5 35.8 %copy-start.4 = (f32[2,16,8,128]{3,2,1,0:T(8,128)S(1)}, f32[2,16,8,128]{3,2,1,0:T(8,128)}, u32[]{:S(2)}) copy-start(f32[2,16,8,128]{3,2,1,0:T(8,128)} %constant.18.clone.refs_3_) | copy-start | bytes 393220
  2.5 35.8 %copy-start.6 = (f32[2,4,1,128]{3,2,1,0:T(1,128)S(1)}, f32[2,4,1,128]{3,2,1,0:T(1,128)}, u32[]{:S(2)}) copy-start(f32[2,4,1,128]{3,2,1,0:T(1,128)} %constant.17.clone.refs_2_) | copy-start | bytes 12292
  2.5 35.8 %copy-start.7 = (s32[4]{0:T(128)S(1)}, s32[4]{0:T(128)}, u32[]{:S(2)}) copy-start(s32[4]{0:T(128)} %refs_0_.3) | copy-start | bytes 52
  40.7 27.7 %copy-start.5 = (bf16[256,256]{1,0:T(8,128)(2,1)S(1)}, bf16[256,256]{1,0:T(8,128)(2,1)}, u32[]{:S(2)}) copy-start(bf16[256,256]{1,0:T(8,128)(2,1)} %constant.23.clone.refs_1_) | copy-start | bytes 393220

commit v5 on v4

--- a/solution.py
+++ b/solution.py
@@ -78,45 +78,38 @@
     contract = ((1,), (1,))
     group = LANES // n.q
     width = n.entries * n.q
-    steps = min(4, n.tiles)
-    per = n.tiles // steps
-    loads = [pltpu.make_async_copy(weights_hbm, weights, sems.at[0])]
-    for s in range(steps):
-        part = pl.ds(s * per * group, per * group)
-        loads.append(pltpu.make_async_copy(dense_hbm.at[part], dense.at[part], sems.at[1 + s]))
-    loads.append(pltpu.make_async_copy(sparse_hbm, sparse, sems.at[1 + steps]))
+    loads = [
+        pltpu.make_async_copy(weights_hbm, weights, sems.at[0]),
+        pltpu.make_async_copy(sparse_hbm, sparse, sems.at[1]),
+        pltpu.make_async_copy(dense_hbm, dense, sems.at[2]),
+    ]
     for load in loads:
         load.start()
-    loads[0].wait()
-    table = weights[...]
+    for load in loads:
+        load.wait()
+    first, second = weights[:, :n.rows], weights[:, n.rows:]
+    twice = jnp.concatenate([first, first], axis=1)
     me = lax.axis_index("sub")
 
     def slots_of(rows):
         high, low = split(rows)
         both = jnp.concatenate([high, low], axis=1)
         dot = lambda x, y: lax.dot_general(x, y, (contract, ((), ())), preferred_element_type=jnp.float32)
-        return dot(table[:, :2 * n.rows], both) + dot(table[:, 2 * n.rows:], high)
-
-    for s in range(steps):
-        loads[1 + s].wait()
-        rows = [
-            dense[t * group + lax.rem(g - me + group, group)]
-            for t in range(s * per, (s + 1) * per) for g in range(group)
-        ]
-        slots = slots_of(jnp.concatenate(rows, axis=0))
-        for i in range(per):
-            t = s * per + i
-            for d in range(n.devices):
-                for c in range(2):
-                    rows = slice((d * 2 + c) * nf, (d * 2 + c + 1) * nf)
-                    out_ref[d, c * n.tiles + t] = slots[rows, i * LANES:(i + 1) * LANES]
-    loads[-1].wait()
-    slots = slots_of(sparse[...].reshape(width, n.rows))
+        return dot(twice, both) + dot(second, high)
+
+    few = slots_of(sparse[...].reshape(width, n.rows))
     for d in range(n.devices):
-        pieces = [slots[(d * 2 + c) * nf:(d * 2 + c + 1) * nf] for c in range(2)]
+        pieces = [few[(d * 2 + c) * nf:(d * 2 + c + 1) * nf] for c in range(2)]
         if 2 * width < LANES:
             pieces.append(jnp.zeros((nf, LANES - 2 * width), jnp.float32))
         out_ref[d, 2 * n.tiles] = jnp.concatenate(pieces, axis=1)
+    rows = [dense[t * group + lax.rem(g - me + group, group)] for t in range(n.tiles) for g in range(group)]
+    slots = slots_of(jnp.concatenate(rows, axis=0))
+    for t in range(n.tiles):
+        for d in range(n.devices):
+            for c in range(2):
+                at = slice((d * 2 + c) * nf, (d * 2 + c + 1) * nf)
+                out_ref[d, c * n.tiles + t] = slots[at, t * LANES:(t + 1) * LANES]
 
 
 RUN = 8
@@ -276,16 +269,15 @@
         whole = pl.BlockSpec(memory_space=pltpu.VMEM)
         out = lambda *shape: jax.ShapeDtypeStruct(shape, jnp.float32)
         hbm = pl.BlockSpec(memory_space=pltpu.HBM)
-        steps = min(4, n.tiles)
         high, low = halves(forward)
-        table = np.concatenate([high, high, low], axis=1)
+        table = np.concatenate([high, low], axis=1)
         sent = pl.pallas_call(
             lambda *refs: rows_to_slots(n, *refs),
             out_shape=pltpu.VMEM((n.devices, 2 * n.tiles + 1, n.nf, LANES), jnp.float32),
             in_specs=[hbm] * 3, out_specs=whole, name="rows_to_slots", compiler_params=GRANT,
             scratch_shapes=[
                 pltpu.VMEM(dense.shape, jnp.float32), pltpu.VMEM(sparse.shape, jnp.float32),
-                pltpu.VMEM((2 * n.rows, 3 * n.rows), jnp.bfloat16), pltpu.SemaphoreType.DMA((steps + 2,)),
+                pltpu.VMEM((2 * n.rows, 2 * n.rows), jnp.bfloat16), pltpu.SemaphoreType.DMA((3,)),
             ],
         )(*(pltpu.with_memory_space_constraint(v, pltpu.HBM) for v in (dense, sparse, jnp.asarray(table))))
         taken = lax.all_to_all(sent, AXES, 0, 0, tiled=True)

time: 70.3 us -> 69.4 us (0.987)
  Pallas kernels: 5.94 us -> 5.13 us
    pallas_call x1, Pallas kernels: 2.45 us -> 1.63 us  [local(): pl.pallas_call(lambda *refs: rows_to_slots(n, *refs), out_shape=pltpu.VME...]
where the time goes in v5:
time: 69.4 us; the launch traced here: 68.7 us
  blocking collectives  63.4 us (91%)
  Pallas kernels  5.13 us (7%)
    all_to_all x1, blocking collectives, local(): taken = lax.all_to_all(sent, AXES, 0, 0, tiled=True)  35.8 us
    all_to_all x1, blocking collectives, local(): back = lax.all_to_all(mixed, AXES, 0, 0, tiled=True)  27.7 us
    pallas_call x1, Pallas kernels, local(): pl.pallas_call(lambda *refs: middle(n, *refs), out_shape=out(n.devices, 2...  2.32 us
    pallas_call x1, Pallas kernels, local(): pl.pallas_call(lambda *refs: rows_to_slots(n, *refs), out_shape=pltpu.VME...  1.63 us

profile of v5, /device:TPU:0, one launch (start us, length us, event | category | flops | bytes accessed | tf_op | source)
XLA Modules:
  0.0 68.7 jit_solution(1450102017518347072)
XLA Ops:
  0.0 1.6 %rows_to_slots.1 = f32[16,17,8,128]{3,2,1,0:T(8,128)S(1)} custom-call(f32[32,32,128]{2,1,0:T(8,128)} %refs_0_.2, f32[1,32,128]{2,1,0:T(8,128)} %refs_1_.2, bf16[256,256]{1,0:T(8,128)(2,1)} %constant.16.clone.refs_2_), custom_call_target="tpu_custom_call" | custom-call | tf_op jit(solution)/shard_map/rows_to_slots/pallas_call | solution.py:274
  1.6 0.0 copy-start
  1.7 0.0 copy-start.1
  1.7 0.0 copy-start.2
  1.7 0.0 copy-start.3
  1.7 0.0 copy-start.4
  1.7 0.0 copy-start.6
  1.7 0.0 copy-start.7
  1.7 35.8 %all_to_all.10.refs_1_ = f32[16,17,8,128]{3,2,1,0:T(8,128)S(1)} all-to-all(f32[16,17,8,128]{3,2,1,0:T(8,128)S(1)} %rows_to_slots.1), channel_id=1, replica_groups=mesh['groups'=2,'blk'=4,'sub'=4] {'blk','sub'}, dimensions={0} | all-to-all | bytes 2228224 | tf_op jit(solution)/shard_map/all_to_all | solution.py:283
  37.5 0.0 copy-done
  37.5 0.0 copy-done.1
  37.5 0.0 copy-done.2
  37.5 0.0 copy-done.3
  37.5 0.0 copy-done.4
  37.5 0.0 copy-done.6
  37.5 0.0 copy-done.7
  37.6 2.3 %middle.1 = f32[16,16,8,128]{3,2,1,0:T(8,128)S(1)} custom-call(s32[4]{0:T(128)S(1)} %copy-done.7, f32[16,17,8,128]{3,2,1,0:T(8,128)S(1)} %all_to_all.10.refs_1_, f32[2,4,1,128]{3,2,1,0:T(1,128)S(1)} %copy-done.6, f32[2,16,8,128]{3,2,1,0:T(8,128)S(1)} %copy-done.4, bf16[256,256]{1,0:T(8,128)(2,1)S(1)} %copy-done.3, bf16[256,256]{1,0:T(8,128)(2,1)S(1)} %copy-done.2, ...), custom_call_target="tpu_custom_call" | custom-call | tf_op jit(solution)/shard_map/middle/pallas_call | solution.py:284
  39.9 0.0 copy-start.5
  39.9 27.7 %all_to_all.11.refs_0_ = f32[16,16,8,128]{3,2,1,0:T(8,128)S(1)} all-to-all(f32[16,16,8,128]{3,2,1,0:T(8,128)S(1)} %middle.1), channel_id=1, replica_groups=mesh['groups'=2,'blk'=4,'sub'=4] {'blk','sub'}, dimensions={0} | all-to-all | bytes 2097152 | tf_op jit(solution)/shard_map/all_to_all | solution.py:293
  67.6 0.0 copy-done.5
  67.6 1.2 %slots_to_rows.1 = f32[32,32,128]{2,1,0:T(8,128)} custom-call(f32[16,16,8,128]{3,2,1,0:T(8,128)S(1)} %all_to_all.11.refs_0_, bf16[256,256]{1,0:T(8,128)(2,1)S(1)} %copy-done.5), custom_call_target="tpu_custom_call" | custom-call | tf_op jit(solution)/shard_map/slots_to_rows/pallas_call | solution.py:294
Async XLA Ops:
  1.6 35.9 %copy-start = (bf16[256,256]{1,0:T(8,128)(2,1)S(1)}, bf16[256,256]{1,0:T(8,128)(2,1)}, u32[]{:S(2)}) copy-start(bf16[256,256]{1,0:T(8,128)(2,1)} %constant.22.clone.refs_7_) | copy-start | bytes 393220
  1.7 35.9 %copy-start.1 = (bf16[256,256]{1,0:T(8,128)(2,1)S(1)}, bf16[256,256]{1,0:T(8,128)(2,1)}, u32[]{:S(2)}) copy-start(bf16[256,256]{1,0:T(8,128)(2,1)} %constant.21.clone.refs_6_) | copy-start | bytes 393220
  1.7 35.9 %copy-start.2 = (bf16[256,256]{1,0:T(8,128)(2,1)S(1)}, bf16[256,256]{1,0:T(8,128)(2,1)}, u32[]{:S(2)}) copy-start(bf16[256,256]{1,0:T(8,128)(2,1)} %constant.20.clone.refs_5_) | copy-start | bytes 393220
  1.7 35.8 %copy-start.3 = (bf16[256,256]{1,0:T(8,128)(2,1)S(1)}, bf16[256,256]{1,0:T(8,128)(2,1)}, u32[]{:S(2)}) copy-start(bf16[256,256]{1,0:T(8,128)(2,1)} %constant.19.clone.refs_4_) | copy-start | bytes 393220
  1.7 35.8 %copy-start.4 = (f32[2,16,8,128]{3,2,1,0:T(8,128)S(1)}, f32[2,16,8,128]{3,2,1,0:T(8,128)}, u32[]{:S(2)}) copy-start(f32[2,16,8,128]{3,2,1,0:T(8,128)} %constant.18.clone.refs_3_) | copy-start | bytes 393220
  1.7 35.8 %copy-start.6 = (f32[2,4,1,128]{3,2,1,0:T(1,128)S(1)}, f32[2,4,1,128]{3,2,1,0:T(1,128)}, u32[]{:S(2)}) copy-start(f32[2,4,1,128]{3,2,1,0:T(1,128)} %constant.17.clone.refs_2_) | copy-start | bytes 12292
  1.7 35.8 %copy-start.7 = (s32[4]{0:T(128)S(1)}, s32[4]{0:T(128)}, u32[]{:S(2)}) copy-start(s32[4]{0:T(128)} %refs_0_.3) | copy-start | bytes 52
  39.9 27.7 %copy-start.5 = (bf16[256,256]{1,0:T(8,128)(2,1)S(1)}, bf16[256,256]{1,0:T(8,128)(2,1)}, u32[]{:S(2)}) copy-start(bf16[256,256]{1,0:T(8,128)(2,1)} %constant.23.clone.refs_1_) | copy-start | bytes 393220

commit v6 on v5

--- a/solution.py
+++ b/solution.py
@@ -52,6 +52,9 @@
         self.nf = self.rows // self.devices
         self.tiles = self.blocks * self.q // LANES
         self.all_blocks = self.blocks * self.z
+        self.parts = 2 if self.nf % 2 == 0 and 4 * self.entries * self.q <= LANES else 1
+        self.height = self.nf // self.parts
+        self.pieces = (2 * self.tiles) * self.parts + 1
 
 
 def tables(n):
@@ -99,17 +102,23 @@
 
     few = slots_of(sparse[...].reshape(width, n.rows))
     for d in range(n.devices):
-        pieces = [few[(d * 2 + c) * nf:(d * 2 + c + 1) * nf] for c in range(2)]
-        if 2 * width < LANES:
-            pieces.append(jnp.zeros((nf, LANES - 2 * width), jnp.float32))
-        out_ref[d, 2 * n.tiles] = jnp.concatenate(pieces, axis=1)
+        pieces = []
+        for p in range(n.parts):
+            for c in range(2):
+                at = (d * 2 + c) * nf + p * n.height
+                pieces.append(few[at:at + n.height])
+        if 2 * n.parts * width < LANES:
+            pieces.append(jnp.zeros((n.height, LANES - 2 * n.parts * width), jnp.float32))
+        out_ref[d, n.pieces - 1] = jnp.concatenate(pieces, axis=1)
     rows = [dense[t * group + lax.rem(g - me + group, group)] for t in range(n.tiles) for g in range(group)]
     slots = slots_of(jnp.concatenate(rows, axis=0))
     for t in range(n.tiles):
         for d in range(n.devices):
             for c in range(2):
-                at = slice((d * 2 + c) * nf, (d * 2 + c + 1) * nf)
-                out_ref[d, c * n.tiles + t] = slots[at, t * LANES:(t + 1) * LANES]
+                at = (d * 2 + c) * nf
+                tile = slots[at:at + nf, t * LANES:(t + 1) * LANES]
+                first_piece = (c * n.tiles + t) * n.parts
+                out_ref[d, first_piece:first_piece + n.parts] = tile.reshape(n.parts, n.height, LANES)
 
 
 RUN = 8
@@ -133,18 +142,25 @@
         rows = wave[at:at + count].reshape(count * nf, 2 * LANES)
         return product3(split(rows), table, contract).reshape(count, nf, 2 * LANES)
 
+    def tile(source, i):
+        return in_ref[source, i * n.parts:(i + 1) * n.parts].reshape(nf, LANES)
+
     def gather(z):
         if z == 0:
             for y in range(n.z):
-                parts = [in_ref[y * n.subs + s, 2 * n.tiles] for s in range(group)]
+                few = [in_ref[y * n.subs + s, n.pieces - 1] for s in range(group)]
                 for e in range(n.entries):
-                    at = e * n.q
-                    re = jnp.concatenate([p[:, at:at + n.q] for p in parts], axis=1)
-                    im = jnp.concatenate([p[:, width + at:width + at + n.q] for p in parts], axis=1)
+                    re, im = (
+                        jnp.concatenate([
+                            jnp.concatenate([
+                                v[:, (p * 2 + c) * width + e * n.q:(p * 2 + c) * width + (e + 1) * n.q]
+                                for v in few], axis=1)
+                            for p in range(n.parts)], axis=0)
+                        for c in range(2))
                     store(y * n.entries + e, re, im)
         for t in range(n.tiles):
-            re = regroup([in_ref[z * n.subs + s, t] for s in range(group)], n.q)
-            im = regroup([in_ref[z * n.subs + s, n.tiles + t] for s in range(group)], n.q)
+            re = regroup([tile(z * n.subs + s, t) for s in range(group)], n.q)
+            im = regroup([tile(z * n.subs + s, n.tiles + t) for s in range(group)], n.q)
             for j in range(group):
                 store(base + z * n.blocks + t * group + j, re[j], im[j], j)
 
@@ -224,10 +240,10 @@
                 er, ei = result[t * group + j, :, :LANES], result[t * group + j, :, LANES:]
                 re.append(er * tc + ei * ts)
                 im.append(ei * tc - er * ts)
-            for s, tile in enumerate(regroup(re, n.q)):
-                out_ref[z * n.subs + s, t] = tile
-            for s, tile in enumerate(regroup(im, n.q)):
-                out_ref[z * n.subs + s, n.tiles + t] = tile
+            for s, value in enumerate(regroup(re, n.q)):
+                out_ref[z * n.subs + s, t] = value
+            for s, value in enumerate(regroup(im, n.q)):
+                out_ref[z * n.subs + s, n.tiles + t] = value
 
     before = convolved(starts(n.all_blocks - 1), 0, factors())
     before = convolve(0, before)
@@ -273,7 +289,7 @@
         table = np.concatenate([high, low], axis=1)
         sent = pl.pallas_call(
             lambda *refs: rows_to_slots(n, *refs),
-            out_shape=pltpu.VMEM((n.devices, 2 * n.tiles + 1, n.nf, LANES), jnp.float32),
+            out_shape=out(n.devices, n.pieces, n.height, LANES),
             in_specs=[hbm] * 3, out_specs=whole, name="rows_to_slots", compiler_params=GRANT,
             scratch_shapes=[
                 pltpu.VMEM(dense.shape, jnp.float32), pltpu.VMEM(sparse.shape, jnp.float32),

time: 69.4 us -> 68.9 us (level)
  no operation moved by 1% of the time
where the time goes in v6:
time: 68.9 us; the launch traced here: 68.2 us
  blocking collectives  62.8 us (91%)
  Pallas kernels  5.22 us (8%)
    all_to_all x1, blocking collectives, local(): taken = lax.all_to_all(sent, AXES, 0, 0, tiled=True)  35.2 us
    all_to_all x1, blocking collectives, local(): back = lax.all_to_all(mixed, AXES, 0, 0, tiled=True)  27.6 us
    pallas_call x1, Pallas kernels, local(): pl.pallas_call(lambda *refs: middle(n, *refs), out_shape=out(n.devices, 2...  2.4 us
    pallas_call x1, Pallas kernels, local(): pl.pallas_call(lambda *refs: rows_to_slots(n, *refs), out_shape=out(n.dev...  1.63 us

profile of v6, /device:TPU:0, one launch (start us, length us, event | category | flops | bytes accessed | tf_op | source)
XLA Modules:
  0.0 68.2 jit_solution(9041695349073533456)
XLA Ops:
  0.0 1.6 %rows_to_slots.1 = f32[16,33,4,128]{3,2,1,0:T(4,128)S(1)} custom-call(f32[32,32,128]{2,1,0:T(8,128)} %refs_0_.2, f32[1,32,128]{2,1,0:T(8,128)} %refs_1_.2, bf16[256,256]{1,0:T(8,128)(2,1)} %constant.16.clone.refs_2_), custom_call_target="tpu_custom_call" | custom-call | tf_op jit(solution)/shard_map/rows_to_slots/pallas_call | solution.py:290
  1.6 0.0 copy-start
  1.7 0.0 copy-start.1
  1.7 0.0 copy-start.2
  1.7 0.0 copy-start.3
  1.7 0.0 copy-start.4
  1.7 0.0 copy-start.6
  1.7 0.0 copy-start.7
  1.7 35.2 %all_to_all.10.refs_1_ = f32[16,33,4,128]{3,2,1,0:T(4,128)S(1)} all-to-all(f32[16,33,4,128]{3,2,1,0:T(4,128)S(1)} %rows_to_slots.1), channel_id=1, replica_groups=mesh['groups'=2,'blk'=4,'sub'=4] {'blk','sub'}, dimensions={0} | all-to-all | bytes 2162688 | tf_op jit(solution)/shard_map/all_to_all | solution.py:299
  37.0 0.0 copy-done
  37.0 0.0 copy-done.1
  37.0 0.0 copy-done.2
  37.0 0.0 copy-done.3
  37.0 0.0 copy-done.4
  37.0 0.0 copy-done.6
  37.0 0.0 copy-done.7
  37.0 2.4 %middle.1 = f32[16,16,8,128]{3,2,1,0:T(8,128)S(1)} custom-call(s32[4]{0:T(128)S(1)} %copy-done.7, f32[16,33,4,128]{3,2,1,0:T(4,128)S(1)} %all_to_all.10.refs_1_, f32[2,4,1,128]{3,2,1,0:T(1,128)S(1)} %copy-done.6, f32[2,16,8,128]{3,2,1,0:T(8,128)S(1)} %copy-done.4, bf16[256,256]{1,0:T(8,128)(2,1)S(1)} %copy-done.3, bf16[256,256]{1,0:T(8,128)(2,1)S(1)} %copy-done.2, ...), custom_call_target="tpu_custom_call" | custom-call | tf_op jit(solution)/shard_map/middle/pallas_call | solution.py:300
  39.4 0.0 copy-start.5
  39.4 27.6 %all_to_all.11.refs_0_ = f32[16,16,8,128]{3,2,1,0:T(8,128)S(1)} all-to-all(f32[16,16,8,128]{3,2,1,0:T(8,128)S(1)} %middle.1), channel_id=1, replica_groups=mesh['groups'=2,'blk'=4,'sub'=4] {'blk','sub'}, dimensions={0} | all-to-all | bytes 2097152 | tf_op jit(solution)/shard_map/all_to_all | solution.py:309
  67.0 0.0 copy-done.5
  67.0 1.2 %slots_to_rows.1 = f32[32,32,128]{2,1,0:T(8,128)} custom-call(f32[16,16,8,128]{3,2,1,0:T(8,128)S(1)} %all_to_all.11.refs_0_, bf16[256,256]{1,0:T(8,128)(2,1)S(1)} %copy-done.5), custom_call_target="tpu_custom_call" | custom-call | tf_op jit(solution)/shard_map/slots_to_rows/pallas_call | solution.py:310
Async XLA Ops:
  1.6 35.3 %copy-start = (bf16[256,256]{1,0:T(8,128)(2,1)S(1)}, bf16[256,256]{1,0:T(8,128)(2,1)}, u32[]{:S(2)}) copy-start(bf16[256,256]{1,0:T(8,128)(2,1)} %constant.22.clone.refs_7_) | copy-start | bytes 393220
  1.7 35.3 %copy-start.1 = (bf16[256,256]{1,0:T(8,128)(2,1)S(1)}, bf16[256,256]{1,0:T(8,128)(2,1)}, u32[]{:S(2)}) copy-start(bf16[256,256]{1,0:T(8,128)(2,1)} %constant.21.clone.refs_6_) | copy-start | bytes 393220
  1.7 35.3 %copy-start.2 = (bf16[256,256]{1,0:T(8,128)(2,1)S(1)}, bf16[256,256]{1,0:T(8,128)(2,1)}, u32[]{:S(2)}) copy-start(bf16[256,256]{1,0:T(8,128)(2,1)} %constant.20.clone.refs_5_) | copy-start | bytes 393220
  1.7 35.3 %copy-start.3 = (bf16[256,256]{1,0:T(8,128)(2,1)S(1)}, bf16[256,256]{1,0:T(8,128)(2,1)}, u32[]{:S(2)}) copy-start(bf16[256,256]{1,0:T(8,128)(2,1)} %constant.19.clone.refs_4_) | copy-start | bytes 393220
  1.7 35.3 %copy-start.4 = (f32[2,16,8,128]{3,2,1,0:T(8,128)S(1)}, f32[2,16,8,128]{3,2,1,0:T(8,128)}, u32[]{:S(2)}) copy-start(f32[2,16,8,128]{3,2,1,0:T(8,128)} %constant.18.clone.refs_3_) | copy-start | bytes 393220
  1.7 35.3 %copy-start.6 = (f32[2,4,1,128]{3,2,1,0:T(1,128)S(1)}, f32[2,4,1,128]{3,2,1,0:T(1,128)}, u32[]{:S(2)}) copy-start(f32[2,4,1,128]{3,2,1,0:T(1,128)} %constant.17.clone.refs_2_) | copy-start | bytes 12292
  1.7 35.3 %copy-start.7 = (s32[4]{0:T(128)S(1)}, s32[4]{0:T(128)}, u32[]{:S(2)}) copy-start(s32[4]{0:T(128)} %refs_0_.3) | copy-start | bytes 52
  39.4 27.6 %copy-start.5 = (bf16[256,256]{1,0:T(8,128)(2,1)S(1)}, bf16[256,256]{1,0:T(8,128)(2,1)}, u32[]{:S(2)}) copy-start(bf16[256,256]{1,0:T(8,128)(2,1)} %constant.23.clone.refs_1_) | copy-start | bytes 393220

commit v7 on v6

--- a/solution.py
+++ b/solution.py
@@ -86,7 +86,7 @@
         pltpu.make_async_copy(sparse_hbm, sparse, sems.at[1]),
         pltpu.make_async_copy(dense_hbm, dense, sems.at[2]),
     ]
-    for load in loads:
+    for load in reversed(loads):
         load.start()
     for load in loads:
         load.wait()

time: 68.9 us -> 68.8 us (level)
  no operation moved by 1% of the time
where the time goes in v7:
time: 68.8 us; the launch traced here: 68.1 us
  blocking collectives  62.8 us (91%)
  Pallas kernels  5.14 us (7%)
    all_to_all x1, blocking collectives, local(): taken = lax.all_to_all(sent, AXES, 0, 0, tiled=True)  35.2 us
    all_to_all x1, blocking collectives, local(): back = lax.all_to_all(mixed, AXES, 0, 0, tiled=True)  27.6 us
    pallas_call x1, Pallas kernels, local(): pl.pallas_call(lambda *refs: middle(n, *refs), out_shape=out(n.devices, 2...  2.38 us
    pallas_call x1, Pallas kernels, local(): pl.pallas_call(lambda *refs: rows_to_slots(n, *refs), out_shape=out(n.dev...  1.58 us

profile of v7, /device:TPU:0, one launch (start us, length us, event | category | flops | bytes accessed | tf_op | source)
XLA Modules:
  0.0 68.1 jit_solution(8896480130164581267)
XLA Ops:
  0.0 1.6 %rows_to_slots.1 = f32[16,33,4,128]{3,2,1,0:T(4,128)S(1)} custom-call(f32[32,32,128]{2,1,0:T(8,128)} %refs_0_.2, f32[1,32,128]{2,1,0:T(8,128)} %refs_1_.2, bf16[256,256]{1,0:T(8,128)(2,1)} %constant.16.clone.refs_2_), custom_call_target="tpu_custom_call" | custom-call | tf_op jit(solution)/shard_map/rows_to_slots/pallas_call | solution.py:290
  1.6 0.0 copy-start
  1.6 0.0 copy-start.1
  1.6 0.0 copy-start.2
  1.6 0.0 copy-start.3
  1.6 0.0 copy-start.4
  1.7 0.0 copy-start.6
  1.7 0.0 copy-start.7
  1.7 35.2 %all_to_all.10.refs_1_ = f32[16,33,4,128]{3,2,1,0:T(4,128)S(1)} all-to-all(f32[16,33,4,128]{3,2,1,0:T(4,128)S(1)} %rows_to_slots.1), channel_id=1, replica_groups=mesh['groups'=2,'blk'=4,'sub'=4] {'blk','sub'}, dimensions={0} | all-to-all | bytes 2162688 | tf_op jit(solution)/shard_map/all_to_all | solution.py:299
  36.9 0.0 copy-done
  36.9 0.0 copy-done.1
  36.9 0.0 copy-done.2
  36.9 0.0 copy-done.3
  36.9 0.0 copy-done.4
  36.9 0.0 copy-done.6
  37.0 0.0 copy-done.7
  37.0 2.4 %middle.1 = f32[16,16,8,128]{3,2,1,0:T(8,128)S(1)} custom-call(s32[4]{0:T(128)S(1)} %copy-done.7, f32[16,33,4,128]{3,2,1,0:T(4,128)S(1)} %all_to_all.10.refs_1_, f32[2,4,1,128]{3,2,1,0:T(1,128)S(1)} %copy-done.6, f32[2,16,8,128]{3,2,1,0:T(8,128)S(1)} %copy-done.4, bf16[256,256]{1,0:T(8,128)(2,1)S(1)} %copy-done.3, bf16[256,256]{1,0:T(8,128)(2,1)S(1)} %copy-done.2, ...), custom_call_target="tpu_custom_call" | custom-call | tf_op jit(solution)/shard_map/middle/pallas_call | solution.py:300
  39.3 0.0 copy-start.5
  39.4 27.6 %all_to_all.11.refs_0_ = f32[16,16,8,128]{3,2,1,0:T(8,128)S(1)} all-to-all(f32[16,16,8,128]{3,2,1,0:T(8,128)S(1)} %middle.1), channel_id=1, replica_groups=mesh['groups'=2,'blk'=4,'sub'=4] {'blk','sub'}, dimensions={0} | all-to-all | bytes 2097152 | tf_op jit(solution)/shard_map/all_to_all | solution.py:309
  67.0 0.0 copy-done.5
  67.0 1.2 %slots_to_rows.1 = f32[32,32,128]{2,1,0:T(8,128)} custom-call(f32[16,16,8,128]{3,2,1,0:T(8,128)S(1)} %all_to_all.11.refs_0_, bf16[256,256]{1,0:T(8,128)(2,1)S(1)} %copy-done.5), custom_call_target="tpu_custom_call" | custom-call | tf_op jit(solution)/shard_map/slots_to_rows/pallas_call | solution.py:310
Async XLA Ops:
  1.6 35.3 %copy-start = (bf16[256,256]{1,0:T(8,128)(2,1)S(1)}, bf16[256,256]{1,0:T(8,128)(2,1)}, u32[]{:S(2)}) copy-start(bf16[256,256]{1,0:T(8,128)(2,1)} %constant.22.clone.refs_7_) | copy-start | bytes 393220
  1.6 35.3 %copy-start.1 = (bf16[256,256]{1,0:T(8,128)(2,1)S(1)}, bf16[256,256]{1,0:T(8,128)(2,1)}, u32[]{:S(2)}) copy-start(bf16[256,256]{1,0:T(8,128)(2,1)} %constant.21.clone.refs_6_) | copy-start | bytes 393220
  1.6 35.3 %copy-start.2 = (bf16[256,256]{1,0:T(8,128)(2,1)S(1)}, bf16[256,256]{1,0:T(8,128)(2,1)}, u32[]{:S(2)}) copy-start(bf16[256,256]{1,0:T(8,128)(2,1)} %constant.20.clone.refs_5_) | copy-start | bytes 393220
  1.6 35.3 %copy-start.3 = (bf16[256,256]{1,0:T(8,128)(2,1)S(1)}, bf16[256,256]{1,0:T(8,128)(2,1)}, u32[]{:S(2)}) copy-start(bf16[256,256]{1,0:T(8,128)(2,1)} %constant.19.clone.refs_4_) | copy-start | bytes 393220
  1.6 35.3 %copy-start.4 = (f32[2,16,8,128]{3,2,1,0:T(8,128)S(1)}, f32[2,16,8,128]{3,2,1,0:T(8,128)}, u32[]{:S(2)}) copy-start(f32[2,16,8,128]{3,2,1,0:T(8,128)} %constant.18.clone.refs_3_) | copy-start | bytes 393220
  1.7 35.3 %copy-start.6 = (f32[2,4,1,128]{3,2,1,0:T(1,128)S(1)}, f32[2,4,1,128]{3,2,1,0:T(1,128)}, u32[]{:S(2)}) copy-start(f32[2,4,1,128]{3,2,1,0:T(1,128)} %constant.17.clone.refs_2_) | copy-start | bytes 12292
  1.7 35.3 %copy-start.7 = (s32[4]{0:T(128)S(1)}, s32[4]{0:T(128)}, u32[]{:S(2)}) copy-start(s32[4]{0:T(128)} %refs_0_.3) | copy-start | bytes 52
  39.3 27.6 %copy-start.5 = (bf16[256,256]{1,0:T(8,128)(2,1)S(1)}, bf16[256,256]{1,0:T(8,128)(2,1)}, u32[]{:S(2)}) copy-start(bf16[256,256]{1,0:T(8,128)(2,1)} %constant.23.clone.refs_1_) | copy-start | bytes 393220

commit v8 on v7

--- a/solution.py
+++ b/solution.py
@@ -84,7 +84,8 @@
     loads = [
         pltpu.make_async_copy(weights_hbm, weights, sems.at[0]),
         pltpu.make_async_copy(sparse_hbm, sparse, sems.at[1]),
-        pltpu.make_async_copy(dense_hbm, dense, sems.at[2]),
+        pltpu.make_async_copy(dense_hbm.at[pl.ds(0, n.blocks // 2)], dense.at[pl.ds(0, n.blocks // 2)], sems.at[2]),
+        pltpu.make_async_copy(dense_hbm.at[pl.ds(n.blocks // 2, n.blocks - n.blocks // 2)], dense.at[pl.ds(n.blocks // 2, n.blocks - n.blocks // 2)], sems.at[3]),
     ]
     for load in reversed(loads):
         load.start()
@@ -293,7 +294,7 @@
             in_specs=[hbm] * 3, out_specs=whole, name="rows_to_slots", compiler_params=GRANT,
             scratch_shapes=[
                 pltpu.VMEM(dense.shape, jnp.float32), pltpu.VMEM(sparse.shape, jnp.float32),
-                pltpu.VMEM((2 * n.rows, 2 * n.rows), jnp.bfloat16), pltpu.SemaphoreType.DMA((3,)),
+                pltpu.VMEM((2 * n.rows, 2 * n.rows), jnp.bfloat16), pltpu.SemaphoreType.DMA((4,)),
             ],
         )(*(pltpu.with_memory_space_constraint(v, pltpu.HBM) for v in (dense, sparse, jnp.asarray(table))))
         taken = lax.all_to_all(sent, AXES, 0, 0, tiled=True)

time: 68.8 us -> 68.8 us (level)
  no operation moved by 1% of the time
where the time goes in v8:
time: 68.8 us; the launch traced here: 68.1 us
  blocking collectives  62.8 us (91%)
  Pallas kernels  5.15 us (7%)
    all_to_all x1, blocking collectives, local(): taken = lax.all_to_all(sent, AXES, 0, 0, tiled=True)  35.2 us
    all_to_all x1, blocking collectives, local(): back = lax.all_to_all(mixed, AXES, 0, 0, tiled=True)  27.6 us
    pallas_call x1, Pallas kernels, local(): pl.pallas_call(lambda *refs: middle(n, *refs), out_shape=out(n.devices, 2...  2.38 us
    pallas_call x1, Pallas kernels, local(): pl.pallas_call(lambda *refs: rows_to_slots(n, *refs), out_shape=out(n.dev...  1.59 us

profile of v8, /device:TPU:0, one launch (start us, length us, event | category | flops | bytes accessed | tf_op | source)
XLA Modules:
  0.0 68.1 jit_solution(3599917289683164412)
XLA Ops:
  0.0 1.6 %rows_to_slots.1 = f32[16,33,4,128]{3,2,1,0:T(4,128)S(1)} custom-call(f32[32,32,128]{2,1,0:T(8,128)} %refs_0_.2, f32[1,32,128]{2,1,0:T(8,128)} %refs_1_.2, bf16[256,256]{1,0:T(8,128)(2,1)} %constant.16.clone.refs_2_), custom_call_target="tpu_custom_call" | custom-call | tf_op jit(solution)/shard_map/rows_to_slots/pallas_call | solution.py:291
  1.6 0.0 copy-start
  1.6 0.0 copy-start.1
  1.6 0.0 copy-start.2
  1.6 0.0 copy-start.3
  1.6 0.0 copy-start.4
  1.7 0.0 copy-start.6
  1.7 0.0 copy-start.7
  1.7 35.2 %all_to_all.10.refs_1_ = f32[16,33,4,128]{3,2,1,0:T(4,128)S(1)} all-to-all(f32[16,33,4,128]{3,2,1,0:T(4,128)S(1)} %rows_to_slots.1), channel_id=1, replica_groups=mesh['groups'=2,'blk'=4,'sub'=4] {'blk','sub'}, dimensions={0} | all-to-all | bytes 2162688 | tf_op jit(solution)/shard_map/all_to_all | solution.py:300
  36.9 0.0 copy-done
  36.9 0.0 copy-done.1
  36.9 0.0 copy-done.2
  36.9 0.0 copy-done.3
  36.9 0.0 copy-done.4
  37.0 0.0 copy-done.6
  37.0 0.0 copy-done.7
  37.0 2.4 %middle.1 = f32[16,16,8,128]{3,2,1,0:T(8,128)S(1)} custom-call(s32[4]{0:T(128)S(1)} %copy-done.7, f32[16,33,4,128]{3,2,1,0:T(4,128)S(1)} %all_to_all.10.refs_1_, f32[2,4,1,128]{3,2,1,0:T(1,128)S(1)} %copy-done.6, f32[2,16,8,128]{3,2,1,0:T(8,128)S(1)} %copy-done.4, bf16[256,256]{1,0:T(8,128)(2,1)S(1)} %copy-done.3, bf16[256,256]{1,0:T(8,128)(2,1)S(1)} %copy-done.2, ...), custom_call_target="tpu_custom_call" | custom-call | tf_op jit(solution)/shard_map/middle/pallas_call | solution.py:301
  39.4 0.0 copy-start.5
  39.4 27.6 %all_to_all.11.refs_0_ = f32[16,16,8,128]{3,2,1,0:T(8,128)S(1)} all-to-all(f32[16,16,8,128]{3,2,1,0:T(8,128)S(1)} %middle.1), channel_id=1, replica_groups=mesh['groups'=2,'blk'=4,'sub'=4] {'blk','sub'}, dimensions={0} | all-to-all | bytes 2097152 | tf_op jit(solution)/shard_map/all_to_all | solution.py:310
  67.0 0.0 copy-done.5
  67.0 1.2 %slots_to_rows.1 = f32[32,32,128]{2,1,0:T(8,128)} custom-call(f32[16,16,8,128]{3,2,1,0:T(8,128)S(1)} %all_to_all.11.refs_0_, bf16[256,256]{1,0:T(8,128)(2,1)S(1)} %copy-done.5), custom_call_target="tpu_custom_call" | custom-call | tf_op jit(solution)/shard_map/slots_to_rows/pallas_call | solution.py:311
Async XLA Ops:
  1.6 35.3 %copy-start = (bf16[256,256]{1,0:T(8,128)(2,1)S(1)}, bf16[256,256]{1,0:T(8,128)(2,1)}, u32[]{:S(2)}) copy-start(bf16[256,256]{1,0:T(8,128)(2,1)} %constant.22.clone.refs_7_) | copy-start | bytes 393220
  1.6 35.3 %copy-start.1 = (bf16[256,256]{1,0:T(8,128)(2,1)S(1)}, bf16[256,256]{1,0:T(8,128)(2,1)}, u32[]{:S(2)}) copy-start(bf16[256,256]{1,0:T(8,128)(2,1)} %constant.21.clone.refs_6_) | copy-start | bytes 393220
  1.6 35.3 %copy-start.2 = (bf16[256,256]{1,0:T(8,128)(2,1)S(1)}, bf16[256,256]{1,0:T(8,128)(2,1)}, u32[]{:S(2)}) copy-start(bf16[256,256]{1,0:T(8,128)(2,1)} %constant.20.clone.refs_5_) | copy-start | bytes 393220
  1.6 35.3 %copy-start.3 = (bf16[256,256]{1,0:T(8,128)(2,1)S(1)}, bf16[256,256]{1,0:T(8,128)(2,1)}, u32[]{:S(2)}) copy-start(bf16[256,256]{1,0:T(8,128)(2,1)} %constant.19.clone.refs_4_) | copy-start | bytes 393220
  1.6 35.3 %copy-start.4 = (f32[2,16,8,128]{3,2,1,0:T(8,128)S(1)}, f32[2,16,8,128]{3,2,1,0:T(8,128)}, u32[]{:S(2)}) copy-start(f32[2,16,8,128]{3,2,1,0:T(8,128)} %constant.18.clone.refs_3_) | copy-start | bytes 393220
  1.7 35.3 %copy-start.6 = (f32[2,4,1,128]{3,2,1,0:T(1,128)S(1)}, f32[2,4,1,128]{3,2,1,0:T(1,128)}, u32[]{:S(2)}) copy-start(f32[2,4,1,128]{3,2,1,0:T(1,128)} %constant.17.clone.refs_2_) | copy-start | bytes 12292
  1.7 35.3 %copy-start.7 = (s32[4]{0:T(128)S(1)}, s32[4]{0:T(128)}, u32[]{:S(2)}) copy-start(s32[4]{0:T(128)} %refs_0_.3) | copy-start | bytes 52
  39.4 27.6 %copy-start.5 = (bf16[256,256]{1,0:T(8,128)(2,1)S(1)}, bf16[256,256]{1,0:T(8,128)(2,1)}, u32[]{:S(2)}) copy-start(bf16[256,256]{1,0:T(8,128)(2,1)} %constant.23.clone.refs_1_) | copy-start | bytes 393220
